TPU v7x, 32 devices: a whole 2x2x4 slice. The times are simulated.
32 devices in a mesh: dp: 8 (over y, x, core), mp: 4 (over z).
Axes of the slice: x: 2, y: 2, z: 4, core: 2. Of those that a mesh axis runs over, the one named last changes fastest.
Arguments:
- block_in: bfloat16 [8192, 1024], P(('dp', 'mp')), may hold values from -6 to 6
- out_grad: bfloat16 [8192, 1024], P(('dp', 'mp')), may hold values from -6 to 6
- slot_group: int32 [8], P('dp'), may hold values from 0 to 1, as said below
- decay_rate: float32 [1024], replicated, may hold values from 0.3 to 12
- norm_gain: float32 [2, 1024], replicated, may hold values from 0.1 to 1.9
- norm_gain_moment_one: float32 [2, 1024], replicated, may hold values from -0.00018310547 to 0.00018310547
- norm_gain_moment_two: float32 [2, 1024], replicated, may hold values from 1.5894572e-09 to 7.947286e-09
- short_kernel: float32 [3, 3, 1024], replicated, may hold values from -3.5 to 3.5
- short_kernel_moment_one: float32 [3, 3, 1024], replicated, may hold values from -0.00018310547 to 0.00018310547
- short_kernel_moment_two: float32 [3, 3, 1024], replicated, may hold values from 1.5894572e-09 to 7.947286e-09
- skip_bias: float32 [1024], replicated, may hold values from -6 to 6
- skip_bias_moment_one: float32 [1024], replicated, may hold values from -0.00018310547 to 0.00018310547
- skip_bias_moment_two: float32 [1024], replicated, may hold values from 1.5894572e-09 to 7.947286e-09
- filter_first: float32 [33, 64], replicated, may hold values from -1 to 1
- filter_first_moment_one: float32 [33, 64], replicated, may hold values from -0.00018310547 to 0.00018310547
- filter_first_moment_two: float32 [33, 64], replicated, may hold values from 1.5894572e-09 to 7.947286e-09
- filter_inner: float32 [2, 64, 64], replicated, may hold values from -0.75 to 0.75
- filter_inner_moment_one: float32 [2, 64, 64], replicated, may hold values from -0.00018310547 to 0.00018310547
- filter_inner_moment_two: float32 [2, 64, 64], replicated, may hold values from 1.5894572e-09 to 7.947286e-09
- filter_last: float32 [64, 1024], replicated, may hold values from -0.109375 to 0.109375
- filter_last_moment_one: float32 [64, 1024], replicated, may hold values from -0.00018310547 to 0.00018310547
- filter_last_moment_two: float32 [64, 1024], replicated, may hold values from 1.5894572e-09 to 7.947286e-09
- in_weight: float32 [3, 1024, 1024], P(None, 'mp', 'dp'), may hold values from -0.1875 to 0.1875
- in_weight_moment_one: float32 [3, 1024, 1024], P(None, 'mp', 'dp'), may hold values from -0.00018310547 to 0.00018310547
- in_weight_moment_two: float32 [3, 1024, 1024], P(None, 'mp', 'dp'), may hold values from 1.5894572e-09 to 7.947286e-09
- out_weight: float32 [1024, 1024], P('mp', 'dp'), may hold values from -0.1875 to 0.1875
- out_weight_moment_one: float32 [1024, 1024], P('mp', 'dp'), may hold values from -0.00018310547 to 0.00018310547
- out_weight_moment_two: float32 [1024, 1024], P('mp', 'dp'), may hold values from 1.5894572e-09 to 7.947286e-09
- up_weight: float32 [4096, 1024], P('mp', 'dp'), may hold values from -0.1875 to 0.1875
- up_weight_moment_one: float32 [4096, 1024], P('mp', 'dp'), may hold values from -0.00018310547 to 0.00018310547
- up_weight_moment_two: float32 [4096, 1024], P('mp', 'dp'), may hold values from 1.5894572e-09 to 7.947286e-09
- down_weight: float32 [4096, 1024], P('mp', 'dp'), may hold values from -0.09375 to 0.09375
- down_weight_moment_one: float32 [4096, 1024], P('mp', 'dp'), may hold values from -0.00018310547 to 0.00018310547
- down_weight_moment_two: float32 [4096, 1024], P('mp', 'dp'), may hold values from 1.5894572e-09 to 7.947286e-09
Outputs:
- block_out: bfloat16 [8192, 1024], P(('dp', 'mp'))
- in_grad: float32 [8192, 1024], P(('dp', 'mp'))
- grad_norm: float32 [], replicated
- norm_gain_update: float32 [2, 1024], replicated
- new_norm_gain_moment_one: float32 [2, 1024], replicated
- new_norm_gain_moment_two: float32 [2, 1024], replicated
- short_kernel_update: float32 [3, 3, 1024], replicated
- new_short_kernel_moment_one: float32 [3, 3, 1024], replicated
- new_short_kernel_moment_two: float32 [3, 3, 1024], replicated
- skip_bias_update: float32 [1024], replicated
- new_skip_bias_moment_one: float32 [1024], replicated
- new_skip_bias_moment_two: float32 [1024], replicated
- filter_first_update: float32 [33, 64], replicated
- new_filter_first_moment_one: float32 [33, 64], replicated
- new_filter_first_moment_two: float32 [33, 64], replicated
- filter_inner_update: float32 [2, 64, 64], replicated
- new_filter_inner_moment_one: float32 [2, 64, 64], replicated
- new_filter_inner_moment_two: float32 [2, 64, 64], replicated
- filter_last_update: float32 [64, 1024], replicated
- new_filter_last_moment_one: float32 [64, 1024], replicated
- new_filter_last_moment_two: float32 [64, 1024], replicated
- in_weight_update: float32 [3, 1024, 1024], P(None, 'mp', 'dp')
- new_in_weight_moment_one: float32 [3, 1024, 1024], P(None, 'mp', 'dp')
- new_in_weight_moment_two: float32 [3, 1024, 1024], P(None, 'mp', 'dp')
- out_weight_update: float32 [1024, 1024], P('mp', 'dp')
- new_out_weight_moment_one: float32 [1024, 1024], P('mp', 'dp')
- new_out_weight_moment_two: float32 [1024, 1024], P('mp', 'dp')
- up_weight_update: float32 [4096, 1024], P('mp', 'dp')
- new_up_weight_moment_one: float32 [4096, 1024], P('mp', 'dp')
- new_up_weight_moment_two: float32 [4096, 1024], P('mp', 'dp')
- down_weight_update: float32 [4096, 1024], P('mp', 'dp')
- new_down_weight_moment_one: float32 [4096, 1024], P('mp', 'dp')
- new_down_weight_moment_two: float32 [4096, 1024], P('mp', 'dp')
Inputs may be any that keep to these rules, and one draw needn't show every extreme that they name: `slot_group`: 0 where a slot is one sequence of 1024 tokens, 1 where it is 4 sequences of 256 tokens; both values occur.
All inputs are finite; a program needn't handle non-finite values.
Results may differ from a plain program's by a relative error of at most 0.007.
The roundings to bfloat16 on the way count: a program that leaves them out, or rounds other values in their place, can miss the bound.
Values may be sent and summed in bfloat16 or wider, within the bound.
A program may use at most 256 MiB of HBM per device.

v0:
```python
import math

import jax
import jax.numpy as jnp
from jax import lax
from jax.sharding import PartitionSpec as P

SHORT = 256
STEP = 10


EPSILON = 1e-05
HIGHEST = lax.Precision.HIGHEST
BETA_ONE = 0.9
BETA_TWO = 0.95
LEARN_RATE = 0.01
WEIGHT_DECAY = 0.1
ADAM_EPSILON = 1e-08
CLIP_NORM = 1.0


def layer_norm(values, gain_row):
    mean_val = jnp.mean(values, axis=-1, keepdims=True)
    centered = values - mean_val
    variance = jnp.mean(centered * centered, axis=-1, keepdims=True)
    return centered * lax.rsqrt(variance + EPSILON) * gain_row


def filter_taps(length, first_layer, inner_layers, last_layer, decay_row):
    position = jnp.arange(length).astype(jnp.float32)
    frequency = jnp.linspace(0.0001, 15.0, 16).astype(jnp.float32)
    angles = 2.0 * math.pi / length * position[:, None] * frequency[None, :]
    embedded = jnp.concatenate(
        [position[:, None] / (length - 1), jnp.cos(angles), -jnp.sin(angles)], axis=1
    )
    hidden = jnp.sin(
        jnp.dot(embedded, first_layer, precision=HIGHEST, preferred_element_type=jnp.float32)
    )
    hidden = jnp.sin(
        jnp.dot(hidden, inner_layers[0], precision=HIGHEST, preferred_element_type=jnp.float32)
    )
    hidden = jnp.sin(
        jnp.dot(hidden, inner_layers[1], precision=HIGHEST, preferred_element_type=jnp.float32)
    )
    raw_taps = jnp.dot(hidden, last_layer, precision=HIGHEST, preferred_element_type=jnp.float32)
    return raw_taps * jnp.exp(-decay_row[None, :] * position[:, None] / (length - 1))


def split_factor(length_all):
    chosen = 1
    candidate = 1
    while candidate * candidate <= length_all:
        if length_all % candidate == 0:
            chosen = candidate
        candidate += 1
    return chosen


def twiddle(count_one, count_two, modulus, orient):
    index_one = jnp.arange(count_one, dtype=jnp.int32)
    index_two = jnp.arange(count_two, dtype=jnp.int32)
    angles = (index_one[:, None] * index_two[None, :] % modulus).astype(jnp.float32) * (
        2.0 * math.pi / modulus
    )
    return (jnp.cos(angles), orient * jnp.sin(angles))


def transform(real_part, imag_part, orient, want_imag):
    batches, length_all, channels = real_part.shape
    first_len = split_factor(length_all)
    second_len = length_all // first_len
    cos_one, sin_one = twiddle(first_len, first_len, first_len, orient)
    cos_mid, sin_mid = twiddle(first_len, second_len, length_all, orient)
    cos_two, sin_two = twiddle(second_len, second_len, second_len, orient)
    grid_real = real_part.reshape(batches, first_len, second_len, channels)
    step_real = jnp.einsum("kn,snmc->skmc", cos_one, grid_real, precision=HIGHEST)
    step_imag = jnp.einsum("kn,snmc->skmc", sin_one, grid_real, precision=HIGHEST)
    if imag_part is not None:
        grid_imag = imag_part.reshape(batches, first_len, second_len, channels)
        step_real = step_real - jnp.einsum("kn,snmc->skmc", sin_one, grid_imag, precision=HIGHEST)
        step_imag = step_imag + jnp.einsum("kn,snmc->skmc", cos_one, grid_imag, precision=HIGHEST)
    turned_real = step_real * cos_mid[None, :, :, None] - step_imag * sin_mid[None, :, :, None]
    turned_imag = step_real * sin_mid[None, :, :, None] + step_imag * cos_mid[None, :, :, None]
    out_real = jnp.einsum("skmc,mj->skjc", turned_real, cos_two, precision=HIGHEST) - jnp.einsum(
        "skmc,mj->skjc", turned_imag, sin_two, precision=HIGHEST
    )
    out_real = out_real.transpose(0, 2, 1, 3).reshape(batches, length_all, channels)
    if not want_imag:
        return (out_real, None)
    out_imag = jnp.einsum("skmc,mj->skjc", turned_real, sin_two, precision=HIGHEST) + jnp.einsum(
        "skmc,mj->skjc", turned_imag, cos_two, precision=HIGHEST
    )
    out_imag = out_imag.transpose(0, 2, 1, 3).reshape(batches, length_all, channels)
    return (out_real, out_imag)


def fft_conv(signal, filter_rows):
    batches, length, channels = signal.shape
    padding = ((0, 0), (0, length), (0, 0))
    sig_real, sig_imag = transform(jnp.pad(signal, padding), None, -1.0, True)
    tap_real, tap_imag = transform(jnp.pad(filter_rows, padding), None, -1.0, True)
    prod_real = sig_real * tap_real - sig_imag * tap_imag
    prod_imag = sig_real * tap_imag + sig_imag * tap_real
    back_real = transform(prod_real, prod_imag, 1.0, False)[0]
    return back_real[:, :length] / (2 * length)


def mixer_core(
    projected, kernel_taps, skip_row, first_layer, inner_layers, last_layer, decay_row, group_flag
):
    length, parts, channels = projected.shape
    position = jnp.arange(length, dtype=jnp.int32)
    in_seq = jnp.where(group_flag == 0, position, position % SHORT)
    zeros_row = jnp.zeros((1, parts, channels), jnp.float32)
    shift_one = (
        jnp.concatenate([zeros_row, projected[:-1]], 0)
        * (in_seq >= 1).astype(jnp.float32)[:, None, None]
    )
    shift_two = (
        jnp.concatenate([zeros_row, zeros_row, projected[:-2]], 0)
        * (in_seq >= 2).astype(jnp.float32)[:, None, None]
    )
    conved = (
        kernel_taps[:, 0] * projected
        + kernel_taps[:, 1] * shift_one
        + kernel_taps[:, 2] * shift_two
    )
    outer_gate = conved[:, 0]
    gated = conved[:, 2] * conved[:, 1]

    def whole_seq(signal):
        long_taps = filter_taps(length, first_layer, inner_layers, last_layer, decay_row)
        return fft_conv(signal[None], long_taps[None])[0]

    def short_seqs(signal):
        short_taps = filter_taps(SHORT, first_layer, inner_layers, last_layer, decay_row)
        return fft_conv(signal.reshape(length // SHORT, SHORT, channels), short_taps[None]).reshape(
            length, channels
        )

    mixed_sum = lax.cond(group_flag == 0, whole_seq, short_seqs, gated)
    return (mixed_sum + skip_row * gated) * outer_gate


def adam_update(weight, moment_one, moment_two, gradient, clip_scale, decayed):
    clipped = gradient * clip_scale
    new_one = BETA_ONE * moment_one + (1.0 - BETA_ONE) * clipped
    new_two = BETA_TWO * moment_two + (1.0 - BETA_TWO) * clipped * clipped
    change = (
        new_one
        / (1.0 - BETA_ONE**STEP)
        / (jnp.sqrt(new_two / (1.0 - BETA_TWO**STEP)) + ADAM_EPSILON)
    )
    if decayed:
        change = change + WEIGHT_DECAY * weight
    return (-LEARN_RATE * change, new_one, new_two)


def per_device(
    block_in,
    out_grad,
    slot_group,
    decay_rate,
    norm_gain,
    norm_gain_moment_one,
    norm_gain_moment_two,
    short_kernel,
    short_kernel_moment_one,
    short_kernel_moment_two,
    skip_bias,
    skip_bias_moment_one,
    skip_bias_moment_two,
    filter_first,
    filter_first_moment_one,
    filter_first_moment_two,
    filter_inner,
    filter_inner_moment_one,
    filter_inner_moment_two,
    filter_last,
    filter_last_moment_one,
    filter_last_moment_two,
    in_weight,
    in_weight_moment_one,
    in_weight_moment_two,
    out_weight,
    out_weight_moment_one,
    out_weight_moment_two,
    up_weight,
    up_weight_moment_one,
    up_weight_moment_two,
    down_weight,
    down_weight_moment_one,
    down_weight_moment_two,
):
    model_width = block_in.shape[1]
    channels = model_width // lax.axis_size("mp")
    start_chan = lax.axis_index("mp") * channels
    group_flag = slot_group[0]
    contract_last = (((1,), (1,)), ((), ()))
    contract_first = (((0,), (0,)), ((), ()))
    in_low, out_low, up_low, down_low = (
        lax.all_gather(in_weight.astype(jnp.bfloat16), "dp", axis=2, tiled=True),
        lax.all_gather(out_weight.astype(jnp.bfloat16), "dp", axis=1, tiled=True),
        lax.all_gather(up_weight.astype(jnp.bfloat16), "dp", axis=1, tiled=True),
        lax.all_gather(down_weight.astype(jnp.bfloat16), "dp", axis=1, tiled=True),
    )
    residual = block_in.astype(jnp.float32)
    normed_one, norm_one_back = jax.vjp(layer_norm, residual, norm_gain[0])
    normed_full = lax.all_gather(normed_one.astype(jnp.bfloat16), "mp", axis=0, tiled=True)
    projected = jnp.einsum("td,kcd->tkc", normed_full, in_low, preferred_element_type=jnp.float32)
    kern_local = lax.dynamic_slice_in_dim(short_kernel, start_chan, channels, 2)
    skip_local = lax.dynamic_slice_in_dim(skip_bias, start_chan, channels, 0)
    last_local = lax.dynamic_slice_in_dim(filter_last, start_chan, channels, 1)
    decay_local = lax.dynamic_slice_in_dim(decay_rate, start_chan, channels, 0)

    def mixer(proj_in, kern_in, skip_in, first_in, inner_in, last_in):
        return mixer_core(
            proj_in, kern_in, skip_in, first_in, inner_in, last_in, decay_local, group_flag
        )

    mixer_out, mixer_back = jax.vjp(
        mixer, projected, kern_local, skip_local, filter_first, filter_inner, last_local
    )
    mixer_low = mixer_out.astype(jnp.bfloat16)
    picked = mixer_low
    branch = lax.psum_scatter(
        jnp.dot(picked, out_low, preferred_element_type=jnp.float32),
        "mp",
        scatter_dimension=0,
        tiled=True,
    )
    hidden_in = residual + branch
    normed_two, norm_two_back = jax.vjp(layer_norm, hidden_in, norm_gain[1])
    normed_two_low = normed_two.astype(jnp.bfloat16)
    normed_two_full = lax.all_gather(normed_two_low, "mp", axis=0, tiled=True)
    pre_act = lax.dot_general(
        normed_two_full, up_low, contract_last, preferred_element_type=jnp.float32
    )
    activated, gelu_back = jax.vjp(jax.nn.gelu, pre_act)
    activ_low = activated.astype(jnp.bfloat16)
    picked = activ_low
    ffn_out = lax.psum_scatter(
        jnp.dot(picked, down_low, preferred_element_type=jnp.float32),
        "mp",
        scatter_dimension=0,
        tiled=True,
    )
    block_out = (hidden_in + ffn_out).astype(jnp.bfloat16)
    in_back, out_back, up_back, down_back = (
        lax.all_gather(in_weight.astype(jnp.bfloat16), "dp", axis=2, tiled=True),
        lax.all_gather(out_weight.astype(jnp.bfloat16), "dp", axis=1, tiled=True),
        lax.all_gather(up_weight.astype(jnp.bfloat16), "dp", axis=1, tiled=True),
        lax.all_gather(down_weight.astype(jnp.bfloat16), "dp", axis=1, tiled=True),
    )
    cot_full = lax.all_gather(out_grad, "mp", axis=0, tiled=True)
    act_grad = lax.dot_general(
        cot_full, down_back, contract_last, preferred_element_type=jnp.float32
    )
    pre_grad = gelu_back(act_grad)[0].astype(jnp.bfloat16)
    down_grad = lax.dot_general(
        activ_low, cot_full, contract_first, preferred_element_type=jnp.float32
    )
    up_grad = lax.dot_general(
        pre_grad, normed_two_full, contract_first, preferred_element_type=jnp.float32
    )
    picked = pre_grad
    mid_grad = lax.psum_scatter(
        jnp.dot(picked, up_back, preferred_element_type=jnp.float32),
        "mp",
        scatter_dimension=0,
        tiled=True,
    )
    hidden_part, gain_two_grad = norm_two_back(mid_grad)
    hidden_grad = out_grad.astype(jnp.float32) + hidden_part
    hidden_full = lax.all_gather(hidden_grad.astype(jnp.bfloat16), "mp", axis=0, tiled=True)
    mixed_grad = lax.dot_general(
        hidden_full, out_back, contract_last, preferred_element_type=jnp.float32
    )
    out_w_grad = lax.dot_general(
        mixer_low, hidden_full, contract_first, preferred_element_type=jnp.float32
    )
    proj_grad, kern_grad, skip_grad, first_grad, inner_grad, last_grad = mixer_back(mixed_grad)
    proj_low = proj_grad.astype(jnp.bfloat16)
    in_w_grad = jnp.einsum("tkc,td->kcd", proj_low, normed_full, preferred_element_type=jnp.float32)
    picked = proj_low
    normed_one_grad = lax.psum_scatter(
        jnp.einsum("tkc,kcd->td", picked, in_back, preferred_element_type=jnp.float32),
        "mp",
        scatter_dimension=0,
        tiled=True,
    )
    resid_part, gain_one_grad = norm_one_back(normed_one_grad)
    in_grad = hidden_grad + resid_part
    in_w_sum, out_w_sum, up_sum, down_sum = (
        lax.psum_scatter(in_w_grad, "dp", scatter_dimension=2, tiled=True),
        lax.psum_scatter(out_w_grad, "dp", scatter_dimension=1, tiled=True),
        lax.psum_scatter(up_grad, "dp", scatter_dimension=1, tiled=True),
        lax.psum_scatter(down_grad, "dp", scatter_dimension=1, tiled=True),
    )
    gain_grads = jnp.stack([gain_one_grad, gain_two_grad])
    kern_full = lax.dynamic_update_slice_in_dim(
        jnp.zeros_like(short_kernel), kern_grad, start_chan, 2
    )
    skip_full = lax.dynamic_update_slice_in_dim(jnp.zeros_like(skip_bias), skip_grad, start_chan, 0)
    last_full = lax.dynamic_update_slice_in_dim(
        jnp.zeros_like(filter_last), last_grad, start_chan, 1
    )
    big_squares = (
        jnp.sum(in_w_sum * in_w_sum)
        + jnp.sum(out_w_sum * out_w_sum)
        + jnp.sum(up_sum * up_sum)
        + jnp.sum(down_sum * down_sum)
    )
    small_sums = lax.psum(
        (gain_grads, kern_full, skip_full, first_grad, inner_grad, last_full), ("dp", "mp")
    )
    big_total = lax.psum(big_squares, ("dp", "mp"))
    square_total = big_total
    for small_grad in small_sums:
        square_total = square_total + jnp.sum(small_grad * small_grad)
    grad_norm = jnp.sqrt(square_total)
    clip_scale = jnp.minimum(1.0, CLIP_NORM / (grad_norm + 1e-06))
    gradients = (
        small_sums[0],
        small_sums[1],
        small_sums[2],
        small_sums[3],
        small_sums[4],
        small_sums[5],
        in_w_sum,
        out_w_sum,
        up_sum,
        down_sum,
    )
    params = (
        norm_gain,
        short_kernel,
        skip_bias,
        filter_first,
        filter_inner,
        filter_last,
        in_weight,
        out_weight,
        up_weight,
        down_weight,
    )
    firsts = (
        norm_gain_moment_one,
        short_kernel_moment_one,
        skip_bias_moment_one,
        filter_first_moment_one,
        filter_inner_moment_one,
        filter_last_moment_one,
        in_weight_moment_one,
        out_weight_moment_one,
        up_weight_moment_one,
        down_weight_moment_one,
    )
    seconds = (
        norm_gain_moment_two,
        short_kernel_moment_two,
        skip_bias_moment_two,
        filter_first_moment_two,
        filter_inner_moment_two,
        filter_last_moment_two,
        in_weight_moment_two,
        out_weight_moment_two,
        up_weight_moment_two,
        down_weight_moment_two,
    )
    decayed_flags = (False, False, False, True, True, True, True, True, True, True)
    updates = [
        adam_update(
            params[index],
            firsts[index],
            seconds[index],
            gradients[index],
            clip_scale,
            decayed_flags[index],
        )
        for index in range(10)
    ]
    norm_gain_update, new_norm_gain_moment_one, new_norm_gain_moment_two = updates[0]
    short_kernel_update, new_short_kernel_moment_one, new_short_kernel_moment_two = updates[1]
    skip_bias_update, new_skip_bias_moment_one, new_skip_bias_moment_two = updates[2]
    filter_first_update, new_filter_first_moment_one, new_filter_first_moment_two = updates[3]
    filter_inner_update, new_filter_inner_moment_one, new_filter_inner_moment_two = updates[4]
    filter_last_update, new_filter_last_moment_one, new_filter_last_moment_two = updates[5]
    in_weight_update, new_in_weight_moment_one, new_in_weight_moment_two = updates[6]
    out_weight_update, new_out_weight_moment_one, new_out_weight_moment_two = updates[7]
    up_weight_update, new_up_weight_moment_one, new_up_weight_moment_two = updates[8]
    down_weight_update, new_down_weight_moment_one, new_down_weight_moment_two = updates[9]
    return (
        block_out,
        in_grad,
        grad_norm,
        norm_gain_update,
        new_norm_gain_moment_one,
        new_norm_gain_moment_two,
        short_kernel_update,
        new_short_kernel_moment_one,
        new_short_kernel_moment_two,
        skip_bias_update,
        new_skip_bias_moment_one,
        new_skip_bias_moment_two,
        filter_first_update,
        new_filter_first_moment_one,
        new_filter_first_moment_two,
        filter_inner_update,
        new_filter_inner_moment_one,
        new_filter_inner_moment_two,
        filter_last_update,
        new_filter_last_moment_one,
        new_filter_last_moment_two,
        in_weight_update,
        new_in_weight_moment_one,
        new_in_weight_moment_two,
        out_weight_update,
        new_out_weight_moment_one,
        new_out_weight_moment_two,
        up_weight_update,
        new_up_weight_moment_one,
        new_up_weight_moment_two,
        down_weight_update,
        new_down_weight_moment_one,
        new_down_weight_moment_two,
    )


def solution(mesh):
    placed = (
        P(("dp", "mp"), None),
        P(("dp", "mp"), None),
        P("dp"),
        P(),
        P(),
        P(),
        P(),
        P(),
        P(),
        P(),
        P(),
        P(),
        P(),
        P(),
        P(),
        P(),
        P(),
        P(),
        P(),
        P(),
        P(),
        P(),
        P(None, "mp", "dp"),
        P(None, "mp", "dp"),
        P(None, "mp", "dp"),
        P("mp", "dp"),
        P("mp", "dp"),
        P("mp", "dp"),
        P("mp", "dp"),
        P("mp", "dp"),
        P("mp", "dp"),
        P("mp", "dp"),
        P("mp", "dp"),
        P("mp", "dp"),
    )
    return jax.shard_map(
        per_device,
        mesh=mesh,
        in_specs=placed,
        out_specs=(
            P(("dp", "mp"), None),
            P(("dp", "mp"), None),
            P(),
            P(),
            P(),
            P(),
            P(),
            P(),
            P(),
            P(),
            P(),
            P(),
            P(),
            P(),
            P(),
            P(),
            P(),
            P(),
            P(),
            P(),
            P(),
            P(None, "mp", "dp"),
            P(None, "mp", "dp"),
            P(None, "mp", "dp"),
            P("mp", "dp"),
            P("mp", "dp"),
            P("mp", "dp"),
            P("mp", "dp"),
            P("mp", "dp"),
            P("mp", "dp"),
            P("mp", "dp"),
            P("mp", "dp"),
            P("mp", "dp"),
        ),
        check_vma=False,
    )
```

profile of v0, /device:TPU:0, one launch (start us, length us, event | category | flops | bytes accessed | tf_op | source)
XLA Modules:
  0.0 1182.6 jit_solution(5016755224752365679)
XLA Ops:
  20.6 12.5 %all_gather.30 = bf16[256,1024]{1,0:T(8,128)(2,1)} all-gather(bf16[256,128]{1,0:T(8,128)(2,1)S(1)} %convert_element_type.346), channel_id=1, replica_groups=mesh['dp'=8,'mp'=4] {'dp'}, dimensions={1}, use_global_device_ids=true | all-gather | bytes 589824 | tf_op jit(solution)/shard_map/all_gather | solution.py:203
  39.0 47.8 %all-gather.8.cloned.1.call-done = bf16[1024,1024]{1,0:T(8,128)(2,1)} async-done(((bf16[256,1024]{1,0:T(8,128)(2,1)}), bf16[1024,1024]{1,0:T(8,128)(2,1)}) %all-gather.8.cloned.1.call-update) | async-done | bytes 2097168 | tf_op jit(solution)/shard_map/all_gather | solution.py:209
  93.8 89.8 %conditional.2 = (f32[1024,256]{1,0:T(8,128)}, f32[256,33]{0,1:T(8,128)S(1)}, f32[256,64]{0,1:T(8,128)S(1)}, f32[64,64]{1,0:T(8,128)S(1)}, f32[256,64]{0,1:T(8,1...) conditional(s32[]{:T(128)} %convert_element_type.340, ...), branch_computations={%region_2.4_spmd, %region_3.5_spmd} | conditional | flops 5982728704 | bytes 179169856 | solution.py:141
  196.0 100.9 %reduce-scatter.9.cloned.1.call-done = f32[256,1024]{1,0:T(8,128)} async-done(((f32[1024,1024]{1,0:T(8,128)}), f32[256,1024]{1,0:T(8,128)}) %reduce-scatter.9.cloned.1.call-update) | async-done | bytes 1048592 | tf_op jit(solution)/shard_map/reduce_scatter | solution.py:226
  301.0 43.5 %all-gather.18.cloned.1.call-done = bf16[1024,1024]{1,0:T(8,128)(2,1)} async-done(((bf16[256,1024]{1,0:T(8,128)(2,1)}), bf16[1024,1024]{1,0:T(8,128)(2,1)}) %all-gather.18.cloned.1.call-update) | async-done | bytes 2097168 | tf_op jit(solution)/shard_map/all_gather | solution.py:255
  344.5 29.2 %all-gather.16.cloned.1.call-done = bf16[1024,1024]{1,0:T(8,128)(2,1)} async-done(((bf16[1024,128]{1,0:T(8,128)(2,1)}), bf16[1024,1024]{1,0:T(8,128)(2,1)}) %all-gather.16.cloned.1.call-update) | async-done | bytes 2097168 | tf_op jit(solution)/shard_map/all_gather | solution.py:205
  373.7 6.6 fusion.510
  380.4 23.8 %all-gather.14.cloned.1.call-done = bf16[1024,1024]{1,0:T(8,128)(2,1)} async-done(((bf16[1024,128]{1,0:T(8,128)(2,1)}), bf16[1024,1024]{1,0:T(8,128)(2,1)}) %all-gather.14.cloned.1.call-update) | async-done | bytes 2097168 | tf_op jit(solution)/shard_map/all_gather | solution.py:204
  404.2 47.8 %all-gather.12.cloned.1.call-done = bf16[1024,1024]{1,0:T(8,128)(2,1)} async-done(((bf16[256,1024]{1,0:T(8,128)(2,1)}), bf16[1024,1024]{1,0:T(8,128)(2,1)}) %all-gather.12.cloned.1.call-update) | async-done | bytes 2097168 | tf_op jit(solution)/shard_map/all_gather | solution.py:235
  452.0 10.1 fusion.411
  467.9 7.5 fusion.455
  475.7 67.9 %reduce-scatter.13.cloned.1.call-done = f32[256,1024]{1,0:T(8,128)} async-done(((f32[1024,1024]{1,0:T(8,128)}), f32[256,1024]{1,0:T(8,128)}) %reduce-scatter.13.cloned.1.call-update) | async-done | bytes 1048592 | tf_op jit(solution)/shard_map/reduce_scatter | solution.py:267
  546.7 76.5 %reduce-scatter.11.cloned.1.call-done = f32[256,1024]{1,0:T(8,128)} async-done(((f32[1024,1024]{1,0:T(8,128)}), f32[256,1024]{1,0:T(8,128)}) %reduce-scatter.11.cloned.1.call-update) | async-done | bytes 1048592 | tf_op jit(solution)/shard_map/reduce_scatter | solution.py:242
  628.4 6.6 fusion.513
  635.2 8.0 fusion.454
  646.0 28.8 %all-gather.20.cloned.1.call-done = bf16[1024,1024]{1,0:T(8,128)(2,1)} async-done(((bf16[256,1024]{1,0:T(8,128)(2,1)}), bf16[1024,1024]{1,0:T(8,128)(2,1)}) %all-gather.20.cloned.1.call-update) | async-done | bytes 2097168 | tf_op jit(solution)/shard_map/all_gather | solution.py:275
  679.8 92.8 %conditional.3 = (f32[33,64]{1,0:T(8,128)}, f32[2,64,64]{1,2,0:T(8,128)}, f32[64,256]{1,0:T(8,128)}, f32[1024,256]{1,0:T(8,128)}) conditional(s32[]{:T(128)} %convert_element_type.340, (f32[1024,256]{1,0:T(8,128)}, f32[32,32]{0,1:T(8,128)S(1)}, f32[1,16,32,1]{3,2,1,0:T(8,128)}, f32[32,32]{0,1:T(8,128)S(1)}, f32[1,16,32,1]{3,2,1,0:T(8,128)}, ...), branch_computations={%region_11.17_spmd, %region_16.18_spmd} | conditional | flops 6292185088 | bytes 205981568 | solution.py:141
  688.7 6.3 fusion.460
  728.3 7.0 fusion.103
  803.0 131.7 %all-reduce.24.cloned.1.call-done = f32[64,1024]{1,0:T(8,128)} async-done(((f32[64,1024]{1,0:T(8,128)}), f32[64,1024]{1,0:T(8,128)}) %all-reduce.24.cloned.1.call-update) | async-done | bytes 262160 | tf_op jit(solution)/shard_map/psum | solution.py:314
  936.3 36.4 %reduce-scatter.19.cloned.1.call-done = f32[256,128]{1,0:T(8,128)} async-done(((f32[256,1024]{1,0:T(8,128)}), f32[256,128]{1,0:T(8,128)}) %reduce-scatter.19.cloned.1.call-update) | async-done | bytes 131088 | tf_op jit(solution)/shard_map/reduce_scatter | solution.py:296
  974.3 47.8 %reduce-scatter.17.cloned.1.call-done = f32[3,256,128]{2,1,0:T(8,128)} async-done(((f32[3,256,1024]{2,1,0:T(8,128)}), f32[3,256,128]{2,1,0:T(8,128)}) %reduce-scatter.17.cloned.1.call-update) | async-done | bytes 393232 | tf_op jit(solution)/shard_map/reduce_scatter | solution.py:295
  1026.4 74.6 %reduce-scatter.15.cloned.1.call-done = f32[256,1024]{1,0:T(8,128)} async-done(((f32[1024,1024]{1,0:T(8,128)}), f32[256,1024]{1,0:T(8,128)}) %reduce-scatter.15.cloned.1.call-update) | async-done | bytes 1048592 | tf_op jit(solution)/shard_map/reduce_scatter | solution.py:286
  1104.5 44.3 %all-reduce.25 = (f32[]{:T(128)}, f32[2,1024]{1,0:T(2,128)}, f32[3,3,1024]{2,1,0:T(4,128)S(1)}, f32[1024]{0:T(1024)}, f32[33,64]{1,0:T(8,128)S(1)}, /*index=5*/f32[2,64,64]{2,1,0:T(8,128)S(1)}) all-reduce(f32[]{:T(128)S(6)} %add.659, f32[2,1024]{1,0:T(2,128)} %pad_maximum_fusion.5, ...), channel_id=1, replica_groups=mesh['dp'=8,'mp'=4] {'dp','mp'}, use_global_device_ids=true, to_apply=%region_28.30 | all-reduce | flops 22593 | bytes 180744 | tf_op jit(solution)/shard_map/psum | solution.py:317
  (451 shorter events, 258.5 us)
Async XLA Ops:
  7.2 31.8 %all-gather.10.cloned.1.call-start = ((), (), s32[]{:S(2)}) async-start(), calls=%async_computation.9 | async-start | bytes 1769472 | tf_op jit(solution)/shard_map/all_gather | solution.py:202
  9.1 77.8 %all-gather.8.cloned.1.call-start = ((), (), s32[]{:S(2)}) async-start(), calls=%async_computation.8 | async-start | bytes 2621440 | tf_op jit(solution)/shard_map/all_gather | solution.py:209
  14.7 282.1 %reduce-scatter.9.cloned.1.call-start = ((), (), s32[]{:S(2)}) async-start(), calls=%async_computation.10 | async-start | bytes 5242880 | tf_op jit(solution)/shard_map/reduce_scatter | solution.py:226
  191.6 152.9 %all-gather.18.cloned.1.call-start = ((), (), s32[]{:S(2)}) async-start(), calls=%async_computation.15 | async-start | bytes 2621440 | tf_op jit(solution)/shard_map/all_gather | solution.py:255
  192.2 181.5 %all-gather.16.cloned.1.call-start = ((), (), s32[]{:S(2)}) async-start(), calls=%async_computation.13 | async-start | bytes 2359296 | tf_op jit(solution)/shard_map/all_gather | solution.py:205
  194.1 210.1 %all-gather.14.cloned.1.call-start = ((), (), s32[]{:S(2)}) async-start(), calls=%async_computation.12 | async-start | bytes 2359296 | tf_op jit(solution)/shard_map/all_gather | solution.py:204
  195.9 256.1 %all-gather.12.cloned.1.call-start = ((), (), s32[]{:S(2)}) async-start(), calls=%async_computation.11 | async-start | bytes 2621440 | tf_op jit(solution)/shard_map/all_gather | solution.py:235
  300.9 242.6 %reduce-scatter.13.cloned.1.call-start = ((), (), s32[]{:S(2)}) async-start(), calls=%async_computation.16 | async-start | bytes 5242880 | tf_op jit(solution)/shard_map/reduce_scatter | solution.py:267
  467.8 155.4 %reduce-scatter.11.cloned.1.call-start = ((), (), s32[]{:S(2)}) async-start(), calls=%async_computation.14 | async-start | bytes 5242880 | tf_op jit(solution)/shard_map/reduce_scatter | solution.py:242
  475.4 199.3 %all-gather.20.cloned.1.call-start = ((), (), s32[]{:S(2)}) async-start(), calls=%async_computation.17 | async-start | bytes 2621440 | tf_op jit(solution)/shard_map/all_gather | solution.py:275
  628.4 169.1 %reduce-scatter.21.cloned.1.call-start = ((), (), s32[]{:S(2)}) async-start(), calls=%async_computation.21 | async-start | bytes 4718592 | tf_op jit(solution)/shard_map/reduce_scatter | solution.py:297
  635.1 164.2 %reduce-scatter.23.cloned.1.call-start = ((), (), s32[]{:S(2)}) async-start(), calls=%async_computation.22 | async-start | bytes 4718592 | tf_op jit(solution)/shard_map/reduce_scatter | solution.py:298
  643.2 291.5 %all-reduce.24.cloned.1.call-start = ((), (), s32[]{:S(2)}) async-start(), calls=%async_computation.23 | async-start | bytes 524288 | tf_op jit(solution)/shard_map/psum | solution.py:314
  776.7 196.0 %reduce-scatter.19.cloned.1.call-start = ((), (), s32[]{:S(2)}) async-start(), calls=%async_computation.20 | async-start | bytes 1179648 | tf_op jit(solution)/shard_map/reduce_scatter | solution.py:296
  780.3 241.8 %reduce-scatter.17.cloned.1.call-start = ((), (), s32[]{:S(2)}) async-start(), calls=%async_computation.19 | async-start | bytes 3538944 | tf_op jit(solution)/shard_map/reduce_scatter | solution.py:295
  792.2 308.8 %reduce-scatter.15.cloned.1.call-start = ((), (), s32[]{:S(2)}) async-start(), calls=%async_computation.18 | async-start | bytes 5242880 | tf_op jit(solution)/shard_map/reduce_scatter | solution.py:286
  797.4 303.6 %copy-start.8 = (bf16[256,1024]{1,0:T(8,128)(2,1)S(1)}, bf16[256,1024]{1,0:T(8,128)(2,1)}, u32[]{:S(2)}) copy-start(bf16[256,1024]{1,0:T(8,128)(2,1)} %param.40) | copy-start | bytes 1572868
  797.4 303.6 %copy-start.110 = (f32[1,1024]{1,0:T(1,128)S(1)}, f32[1,1024]{1,0:T(1,128)}, u32[]{:S(2)}) copy-start(f32[1,1024]{1,0:T(1,128)} %copy-done.109) | copy-start | bytes 12292
  797.4 303.6 %copy-start.123 = (f32[256]{0:T(256)S(1)}, f32[256]{0:T(256)}, u32[]{:S(2)}) copy-start(f32[256]{0:T(256)} %copy-done.122) | copy-start | bytes 3076
  797.5 305.2 %copy-start.137 = (f32[256]{0:T(256)S(1)}, f32[256]{0:T(256)}, u32[]{:S(2)}) copy-start(f32[256]{0:T(256)} %copy-done.136) | copy-start | bytes 3076
  797.5 305.3 %copy-start.133 = (f32[256]{0:T(256)S(1)}, f32[256]{0:T(256)}, u32[]{:S(2)}) copy-start(f32[256]{0:T(256)} %copy-done.132) | copy-start | bytes 3076
  801.1 302.7 %copy-start.130 = (f32[1024]{0:T(1024)S(1)}, f32[1024]{0:T(1024)}, u32[]{:S(2)}) copy-start(f32[1024]{0:T(1024)} %get-tuple-element.720) | copy-start | bytes 12292
  802.9 355.6 %copy-start.74 = (f32[2,64,64]{2,1,0:T(8,128)S(1)}, f32[2,64,64]{2,1,0:T(8,128)}, u32[]{:S(2)}) copy-start(f32[2,64,64]{2,1,0:T(8,128)} %param.56) | copy-start | bytes 98308
  802.9 355.6 %copy-start.112 = (f32[2,64,64]{2,1,0:T(8,128)S(1)}, f32[2,64,64]{2,1,0:T(8,128)}, u32[]{:S(2)}) copy-start(f32[2,64,64]{2,1,0:T(8,128)} %param.57) | copy-start | bytes 98308
  (109 other events, 1241.8 us)
Sparse Core Ops, SparseCore 0:
  10.5 28.4 all-gather.9
  41.2 45.6 all-gather.7
  191.8 105.0 reduce-scatter.8
  298.3 46.1 all-gather.17
  346.8 26.8 all-gather.15
  376.0 28.0 all-gather.13
  406.3 45.6 all-gather.11
  468.0 75.5 reduce-scatter.12
  545.9 77.2 reduce-scatter.10
  628.5 46.1 all-gather.19
  678.1 49.8 reduce-scatter.20
  731.2 51.0 reduce-scatter.22
  788.4 146.2 all-reduce.23
  937.7 34.9 reduce-scatter.18
  976.0 46.0 reduce-scatter.16
  1024.2 76.7 reduce-scatter.14
where the time goes:
time: 1190 us; the launch traced here: 1180 us
  waiting for transfers between devices  764 us (64%)
  matrix products  172 us (14%)
  other arithmetic  78.3 us (7%)
  blocking collectives  56.8 us (5%)
  local copies, waits for them, and re-layouts  52.5 us (4%)
  loops' own time  33.9 us (3%)
  between operations  24.2 us (2%)
    psum x1, waiting for transfers between devices, per_device(): lax.psum((gain_grads, kern_full, skip_full, first_grad, inner_grad, last_...  132 us
    reduce_scatter x1, waiting for transfers between devices, per_device(): lax.psum_scatter(jnp.dot(picked, out_low, preferred_element_type=jnp.floa...  101 us
    reduce_scatter x1, waiting for transfers between devices, per_device(): lax.psum_scatter(jnp.dot(picked, down_low, preferred_element_type=jnp.flo...  76.5 us
    reduce_scatter x1, waiting for transfers between devices, per_device(): lax.psum_scatter(jnp.einsum('tkc,kcd->td', picked, in_back, preferred_ele...  74.6 us
    reduce_scatter x1, waiting for transfers between devices, per_device(): lax.psum_scatter(jnp.dot(picked, up_back, preferred_element_type=jnp.floa...  67.9 us
    all_gather x1, waiting for transfers between devices, per_device(): lax.all_gather(normed_one.astype(jnp.bfloat16), 'mp', axis=0, tiled=True)  47.8 us
    all_gather x1, waiting for transfers between devices, per_device(): normed_two_full = lax.all_gather(normed_two_low, 'mp', axis=0, tiled=True)  47.8 us
    reduce_scatter x1, waiting for transfers between devices, per_device(): lax.psum_scatter(in_w_grad, 'dp', scatter_dimension=2, tiled=True)  47.8 us
  transfers between devices with their start and end apart: 16, of which 14 were waited for; matrix products, arithmetic and copies ran while one was open for 14% of the time, Pallas kernels for 0%

commit v1 on v0

v1 whole, which is shorter than its diff:
```python
import functools
import math

import jax
import jax.numpy as jnp
from jax import lax
from jax.experimental import pallas as pl
from jax.experimental.pallas import tpu as pltpu
from jax.sharding import PartitionSpec as P

SHORT = 256
STEP = 10
EPSILON = 1e-05
HIGHEST = lax.Precision.HIGHEST
HIGH = lax.Precision.HIGH
BETA_ONE = 0.9
BETA_TWO = 0.95
LEARN_RATE = 0.01
WEIGHT_DECAY = 0.1
ADAM_EPSILON = 1e-08
CLIP_NORM = 1.0
EDGE = 16
LANES = 128
BF = jnp.bfloat16
F32 = jnp.float32
ROWS_ROWS = (((1,), (1,)), ((), ()))
COLS_COLS = (((0,), (0,)), ((), ()))
MESH_IDS = pl.DeviceIdType.MESH


def norm_parts(values):
    mean_val = jnp.mean(values, axis=-1, keepdims=True)
    centered = values - mean_val
    variance = jnp.mean(centered * centered, axis=-1, keepdims=True)
    scale = lax.rsqrt(variance + EPSILON)
    return centered * scale, scale


def norm_back(grad, xhat, scale, gain_row):
    e = grad * gain_row
    mean_e = jnp.mean(e, axis=-1, keepdims=True)
    mean_ex = jnp.mean(e * xhat, axis=-1, keepdims=True)
    return scale * (e - mean_e - xhat * mean_ex), jnp.sum(grad * xhat, axis=0)


def transform_tables(slot, seq_len, tok):
    in_seq = tok % seq_len
    block = tok // seq_len
    inner = 32
    outer = slot // inner
    step = math.pi / (2.0 * seq_len.astype(F32))

    def table(odd):
        turns = (odd[:, None] * in_seq[None, :]) % (4 * seq_len)
        angle = turns.astype(F32) * step
        return jnp.cos(angle), jnp.sin(angle)

    index_a = jnp.arange(outer, dtype=jnp.int32) * inner
    cos_a, sin_a = table(2 * (index_a % seq_len))
    same = (index_a // seq_len)[:, None] == block[None, :]
    cos_a = jnp.where(same, cos_a, 0.0)
    sin_a = jnp.where(same, sin_a, 0.0)
    cos_b, sin_b = table(2 * jnp.arange(inner, dtype=jnp.int32) + 1)
    cos_a, sin_a, cos_b, sin_b = lax.optimization_barrier((cos_a, sin_a, cos_b, sin_b))
    cos_all = cos_a[:, None] * cos_b[None] - sin_a[:, None] * sin_b[None]
    sin_all = sin_a[:, None] * cos_b[None] + cos_a[:, None] * sin_b[None]
    return jnp.concatenate(
        [cos_all.reshape(slot, slot), sin_all.reshape(slot, slot)], axis=0
    )


def embed(seq_len, tok):
    position = (tok % seq_len).astype(F32)
    length = seq_len.astype(F32)
    frequency = jnp.linspace(0.0001, 15.0, 16).astype(F32)
    angles = 2.0 * math.pi / length * position[:, None] * frequency[None, :]
    place = position[:, None] / (length - 1.0)
    return jnp.concatenate([place, jnp.cos(angles), -jnp.sin(angles)], axis=1), place


def filter_taps(embedded, decay, first_layer, inner_layers, last_layer):
    def dense(a, b):
        return jnp.dot(a, b, precision=HIGHEST, preferred_element_type=F32)

    hidden = jnp.sin(dense(embedded, first_layer))
    hidden = jnp.sin(dense(hidden, inner_layers[0]))
    hidden = jnp.sin(dense(hidden, inner_layers[1]))
    return dense(hidden, last_layer) * decay


def adam_update(weight, moment_one, moment_two, gradient, clip_scale, decayed):
    clipped = gradient * clip_scale
    new_one = BETA_ONE * moment_one + (1.0 - BETA_ONE) * clipped
    new_two = BETA_TWO * moment_two + (1.0 - BETA_TWO) * clipped * clipped
    change = (
        new_one
        / (1.0 - BETA_ONE**STEP)
        / (jnp.sqrt(new_two / (1.0 - BETA_TWO**STEP)) + ADAM_EPSILON)
    )
    if decayed:
        change = change + WEIGHT_DECAY * weight
    return (-LEARN_RATE * change, new_one, new_two)


def per_device(
    paths,
    block_in,
    out_grad,
    slot_group,
    decay_rate,
    *state,
):
    names = (
        "norm_gain",
        "short_kernel",
        "skip_bias",
        "filter_first",
        "filter_inner",
        "filter_last",
        "in_weight",
        "out_weight",
        "up_weight",
        "down_weight",
    )
    params = dict(zip(names, state[0::3]))
    firsts = dict(zip(names, state[1::3]))
    seconds = dict(zip(names, state[2::3]))
    norm_gain, short_kernel, skip_bias = (params[n] for n in names[:3])
    filter_first, filter_inner, filter_last = (params[n] for n in names[3:6])

    n_mp = lax.axis_size("mp")
    rows, width = block_in.shape
    slot = rows * n_mp
    wide = 3 * width
    channels = width // n_mp
    mp_at = lax.axis_index("mp")
    start_chan = mp_at * channels
    seq_len = jnp.where(slot_group[0] == 0, slot, SHORT).astype(jnp.int32)
    forward_ring = [(i, i + 1) for i in range(n_mp - 1)]
    backward_ring = [(i + 1, i) for i in range(n_mp - 1)]

    big = [params[n].astype(BF) for n in names[6:]]
    in_full, out_full = paths.gather_mixer(big[0], big[1])
    up_full, down_full = paths.gather_ffn(big[2], big[3])

    edge_in = lax.ppermute(block_in[-EDGE:], "mp", forward_ring)
    tok_ext = jnp.concatenate([edge_in, block_in], axis=0).astype(F32)
    xhat_ext, scale_ext = norm_parts(tok_ext)
    normed_ext = (xhat_ext * norm_gain[0]).astype(BF)
    residual, xhat_one, scale_one = tok_ext[EDGE:], xhat_ext[EDGE:], scale_ext[EDGE:]
    normed_one = normed_ext[EDGE:]
    proj_ext = lax.dot_general(
        normed_ext, in_full.reshape(wide, width), ROWS_ROWS, preferred_element_type=F32
    )
    tok = mp_at * rows + jnp.arange(rows, dtype=jnp.int32)
    pos = tok % seq_len
    kern = [short_kernel[:, j].reshape(1, wide) for j in range(3)]
    shifted = [proj_ext[EDGE:]] + [
        jnp.where((pos >= j)[:, None], proj_ext[EDGE - j : -j], 0.0) for j in (1, 2)
    ]
    conved = kern[0] * shifted[0] + kern[1] * shifted[1] + kern[2] * shifted[2]
    outer, gate, value = (conved[:, k * width : (k + 1) * width] for k in range(3))
    gated = value * gate

    slot_tok = jnp.arange(slot, dtype=jnp.int32)
    table = transform_tables(slot, seq_len, slot_tok)
    embedded, place = embed(seq_len, slot_tok)
    decay_local = lax.dynamic_slice_in_dim(decay_rate, start_chan, channels, 0)
    last_local = lax.dynamic_slice_in_dim(filter_last, start_chan, channels, 1)
    decay = jnp.exp(-decay_local[None, :] * place)
    taps, taps_back = jax.vjp(
        functools.partial(filter_taps, embedded, decay),
        filter_first,
        filter_inner,
        last_local,
    )
    norm_of = 1.0 / seq_len.astype(F32)

    def spectrum(signal):
        both = jnp.dot(table, signal, precision=HIGH, preferred_element_type=F32)
        return both[:slot], both[slot:]

    def signal_of(cos_part, sin_part):
        both = jnp.concatenate([cos_part, sin_part], axis=0)
        return norm_of * lax.dot_general(
            table, both, COLS_COLS, precision=HIGH, preferred_element_type=F32
        )

    def to_channels(values):
        return lax.all_to_all(
            values.astype(BF), "mp", split_axis=1, concat_axis=0, tiled=True
        ).astype(F32)

    def to_tokens(values):
        return lax.all_to_all(
            values.astype(BF), "mp", split_axis=0, concat_axis=1, tiled=True
        ).astype(F32)

    taps_cos, taps_sin = spectrum(taps)
    gated_cos, gated_sin = spectrum(to_channels(gated))
    conv_sum = to_tokens(
        signal_of(
            gated_cos * taps_cos - gated_sin * taps_sin,
            gated_cos * taps_sin + gated_sin * taps_cos,
        )
    )
    mixed = conv_sum + skip_bias * gated
    mixer_low = (mixed * outer).astype(BF)
    hidden_in = residual + jnp.dot(mixer_low, out_full, preferred_element_type=F32)

    xhat_two, scale_two = norm_parts(hidden_in)
    normed_two = (xhat_two * norm_gain[1]).astype(BF)
    pre_act = lax.dot_general(normed_two, up_full, ROWS_ROWS, preferred_element_type=F32)
    activated, gelu_back = jax.vjp(jax.nn.gelu, pre_act)
    activ_low = activated.astype(BF)
    block_out = (
        hidden_in + jnp.dot(activ_low, down_full, preferred_element_type=F32)
    ).astype(BF)
    act_grad = lax.dot_general(out_grad, down_full, ROWS_ROWS, preferred_element_type=F32)
    pre_grad = gelu_back(act_grad)[0].astype(BF)
    ffn_sums = paths.reduce_ffn(
        (pre_grad, normed_two, None), (activ_low, out_grad, None)
    )
    mid_grad = jnp.dot(pre_grad, up_full, preferred_element_type=F32)
    hidden_part, gain_two_grad = norm_back(mid_grad, xhat_two, scale_two, norm_gain[1])
    hidden_grad = out_grad.astype(F32) + hidden_part
    hidden_low = hidden_grad.astype(BF)

    y_grad = lax.dot_general(hidden_low, out_full, ROWS_ROWS, preferred_element_type=F32)
    q_grad = y_grad * outer
    outer_grad = mixed * y_grad
    q_cos, q_sin = spectrum(to_channels(q_grad))
    gated_grad = (
        to_tokens(
            signal_of(
                q_cos * taps_cos + q_sin * taps_sin, q_sin * taps_cos - q_cos * taps_sin
            )
        )
        + skip_bias * q_grad
    )
    taps_grad = signal_of(
        q_cos * gated_cos + q_sin * gated_sin, q_sin * gated_cos - q_cos * gated_sin
    )
    first_grad, inner_grad, last_grad = taps_back(taps_grad)
    skip_grad = jnp.sum(q_grad * gated, axis=0)
    conv_grad = jnp.concatenate(
        [outer_grad, gated_grad * value, gated_grad * gate], axis=1
    )
    edge_grad = lax.ppermute(conv_grad[:8], "mp", backward_ring)
    grad_ext = jnp.concatenate([conv_grad, edge_grad], axis=0)
    pos_ext = (mp_at * rows + jnp.arange(rows + 8, dtype=jnp.int32)) % seq_len
    proj_grad = kern[0] * conv_grad
    for j in (1, 2):
        proj_grad = proj_grad + kern[j] * jnp.where(
            (pos_ext[j : rows + j] >= j)[:, None], grad_ext[j : rows + j], 0.0
        )
    proj_low = proj_grad.astype(BF)
    kern_grad = jnp.stack(
        [jnp.sum(conv_grad * shifted[j], axis=0) for j in range(3)]
    )
    kern_grad = kern_grad.reshape(3, 3, width).transpose(1, 0, 2)
    normed_grad = jnp.dot(
        proj_low, in_full.reshape(wide, width), preferred_element_type=F32
    )
    resid_part, gain_one_grad = norm_back(normed_grad, xhat_one, scale_one, norm_gain[0])
    in_grad = hidden_grad + resid_part

    last_full = lax.dynamic_update_slice_in_dim(
        jnp.zeros_like(filter_last), last_grad, start_chan, 1
    )
    small = (
        jnp.stack([gain_one_grad, gain_two_grad]),
        kern_grad,
        skip_grad,
        first_grad,
        inner_grad,
        last_full,
    )
    gradients, square_total = paths.reduce_mixer(
        (proj_low, normed_one, 3), (mixer_low, hidden_low, None), small, ffn_sums
    )
    grad_norm = jnp.sqrt(square_total)
    clip_scale = jnp.minimum(1.0, CLIP_NORM / (grad_norm + 1e-06))
    outputs = [block_out, in_grad, grad_norm]
    for index, name in enumerate(names):
        outputs.extend(
            adam_update(
                params[name],
                firsts[name],
                seconds[name],
                gradients[index],
                clip_scale,
                index >= 3,
            )
        )
    return tuple(outputs)


def squares(values):
    return sum(jnp.sum(v * v) for v in values)


class PlainPaths:
    def gather(self, shard):
        along = shard.ndim - 1
        part = lax.all_gather(shard, "dp", axis=along, tiled=True)
        return lax.all_gather(part, "mp", axis=along - 1, tiled=True)

    def gather_mixer(self, in_shard, out_shard):
        return self.gather(in_shard), self.gather(out_shard)

    def gather_ffn(self, up_shard, down_shard):
        return self.gather(up_shard), self.gather(down_shard)

    def reduced(self, left, right, parts):
        grad = lax.dot_general(left, right, COLS_COLS, preferred_element_type=F32)
        if parts:
            grad = grad.reshape(parts, -1, grad.shape[-1])
        along = grad.ndim - 1
        part = lax.psum_scatter(grad, "mp", scatter_dimension=along - 1, tiled=True)
        return lax.psum_scatter(part, "dp", scatter_dimension=along, tiled=True)

    def reduce_ffn(self, up_pair, down_pair):
        return self.reduced(*up_pair), self.reduced(*down_pair)

    def reduce_mixer(self, in_pair, out_pair, small, ffn_sums):
        large = (self.reduced(*in_pair), self.reduced(*out_pair)) + tuple(ffn_sums)
        small = lax.psum(small, ("dp", "mp"))
        total = lax.psum(squares(large), ("dp", "mp")) + squares(small)
        return tuple(small) + large, total


def choose_paths(mesh):
    return PlainPaths()


def solution(mesh):
    tokens = P(("dp", "mp"), None)
    weights = (P(None, "mp", "dp"),) * 3 + (P("mp", "dp"),) * 9
    return jax.shard_map(
        functools.partial(per_device, choose_paths(mesh)),
        mesh=mesh,
        in_specs=(tokens, tokens, P("dp"), P()) + (P(),) * 18 + weights,
        out_specs=(tokens, tokens, P()) + (P(),) * 18 + weights,
        check_vma=False,
    )
```

time: 1190 us -> 1900 us (1.60)
  waiting for transfers between devices: 764 us -> 1530 us
  loops' own time: 33.9 us -> 0 us
  local copies, waits for them, and re-layouts: 52.5 us -> 21.3 us
  matrix products: 172 us -> 142 us
  blocking collectives: 56.8 us -> 86.5 us
    reduce_scatter x8, waiting for transfers between devices: 404 us -> 922 us  [the longest x4 741 us: reduced(): part = lax.psum_scatter(grad, 'mp', scatter_dimension=along - 1, tiled=True)]
    all_gather x7, waiting for transfers between devices: 227 us -> 410 us  [the longest x4 333 us: gather(): return lax.all_gather(part, 'mp', axis=along - 1, tiled=True)]
    all_to_all x0 -> x3, waiting for transfers between devices: none -> 78.6 us  [the longest x2 59.5 us: to_tokens(): lax.all_to_all(values.astype(BF), 'mp', split_axis=0, concat_axis=1, tile...]
    another operation x2 -> x0, loops' own time: 33.9 us -> none  [mixer_core(): mixed_sum = lax.cond(group_flag == 0, whole_seq, short_seqs, gated)]
    all_to_all x0 -> x1, blocking collectives: none -> 32.1 us  [to_channels(): lax.all_to_all(values.astype(BF), 'mp', split_axis=1, concat_axis=0, tile...]
    dot_general x59 -> x29, matrix products: 172 us -> 142 us  [the longest x3 34.9 us: signal_of(): lax.dot_general(table, both, COLS_COLS, precision=HIGH, preferred_element...]
  transfers between devices with their start and end apart: 16 -> 21, of which waited for: 14 -> 18; matrix products, arithmetic and copies ran while one was open for 14% -> 9% of each run, Pallas kernels for 0% -> 0%
where the time goes in v1:
time: 1900 us; the launch traced here: 1890 us
  waiting for transfers between devices  1530 us (81%)
  matrix products  142 us (7%)
  blocking collectives  86.5 us (5%)
  other arithmetic  66.2 us (3%)
  between operations  24.8 us (1%)
  local copies, waits for them, and re-layouts  21.3 us (1%)
    reduce_scatter x4, waiting for transfers between devices, reduced(): part = lax.psum_scatter(grad, 'mp', scatter_dimension=along - 1, tiled=True)  741 us
    all_gather x4, waiting for transfers between devices, gather(): return lax.all_gather(part, 'mp', axis=along - 1, tiled=True)  333 us
    reduce_scatter x4, waiting for transfers between devices, reduced(): return lax.psum_scatter(part, 'dp', scatter_dimension=along, tiled=True)  181 us
    psum x1, waiting for transfers between devices, reduce_mixer(): small = lax.psum(small, ('dp', 'mp'))  118 us
    all_gather x3, waiting for transfers between devices, gather(): part = lax.all_gather(shard, 'dp', axis=along, tiled=True)  76.2 us
    all_to_all x2, waiting for transfers between devices, to_tokens(): lax.all_to_all(values.astype(BF), 'mp', split_axis=0, concat_axis=1, tile...  59.5 us
    psum x1, blocking collectives, reduce_mixer(): total = lax.psum(squares(large), ('dp', 'mp')) + squares(small)  43.6 us
  transfers between devices with their start and end apart: 21, of which 18 were waited for; matrix products, arithmetic and copies ran while one was open for 9% of the time, Pallas kernels for 0%

profile of v1, /device:TPU:0, one launch (start us, length us, event | category | flops | bytes accessed | tf_op | source)
XLA Modules:
  0.0 1893.9 jit_solution(2197577764068094764)
XLA Ops:
  12.8 26.2 %all-gather.8.cloned.1.call-done = bf16[3,256,1024]{2,1,0:T(8,128)(2,1)} async-done(((bf16[3,256,128]{2,1,0:T(8,128)(2,1)}), bf16[3,256,1024]{2,1,0:T(8,128)(2,1)}) %all-gather.8.cloned.1.call-update) | async-done | bytes 1572880 | tf_op jit(solution)/shard_map/all_gather | solution.py:306
  39.1 10.9 all_gather.26
  50.1 19.5 %all-gather.18.cloned.1.call-done = bf16[1024,1024]{1,0:T(8,128)(2,1)} async-done(((bf16[1024,128]{1,0:T(8,128)(2,1)}), bf16[1024,1024]{1,0:T(8,128)(2,1)}) %all-gather.18.cloned.1.call-update) | async-done | bytes 2097168 | tf_op jit(solution)/shard_map/all_gather | solution.py:306
  69.7 30.5 %all-gather.14.cloned.1.call-done = bf16[1024,1024]{1,0:T(8,128)(2,1)} async-done(((bf16[1024,128]{1,0:T(8,128)(2,1)}), bf16[1024,1024]{1,0:T(8,128)(2,1)}) %all-gather.14.cloned.1.call-update) | async-done | bytes 2097168 | tf_op jit(solution)/shard_map/all_gather | solution.py:306
  124.8 92.2 %all-gather.10.cloned.1.call-done = bf16[3,1024,1024]{2,1,0:T(8,128)(2,1)} async-done(((bf16[3,256,1024]{2,1,0:T(8,128)(2,1)}), bf16[3,1024,1024]{2,1,0:T(8,128)(2,1)}) %all-gather.10.cloned.1.call-update) | async-done | bytes 6291472 | tf_op jit(solution)/shard_map/all_gather | solution.py:307
  242.4 19.1 %all-to-all-done = bf16[256,4,256]{2,0,1:T(8,128)(2,1)} async-done(((bf16[256,4,256]{2,0,1:T(8,128)(2,1)}), bf16[256,4,256]{2,0,1:T(8,128)(2,1)}, u32[]{:S(2)}, u32[]{:S(2)}) %all-to-all-start) | async-done | bytes 524320 | tf_op jit(solution)/shard_map/all_to_all | solution.py:190
  270.6 17.7 fusion.37
  294.8 30.4 %all-to-all-done.1 = bf16[4,256,256]{2,1,0:T(8,128)(2,1)} async-done(((bf16[4,256,256]{2,1,0:T(8,128)(2,1)}), bf16[4,256,256]{2,1,0:T(8,128)(2,1)}, u32[]{:S(2)}, u32[]{:S(2)}) %all-to-all-start.1) | async-done | bytes 524320 | tf_op jit(solution)/shard_map/all_to_all | solution.py:195
  334.6 99.9 %all-gather.20.cloned.1.call-done = bf16[4096,1024]{1,0:T(8,128)(2,1)} async-done(((bf16[1024,1024]{1,0:T(8,128)(2,1)}), bf16[4096,1024]{1,0:T(8,128)(2,1)}) %all-gather.20.cloned.1.call-update) | async-done | bytes 8388624 | tf_op jit(solution)/shard_map/all_gather | solution.py:307
  442.4 141.4 %all-gather.16.cloned.1.call-done = bf16[4096,1024]{1,0:T(8,128)(2,1)} async-done(((bf16[1024,1024]{1,0:T(8,128)(2,1)}), bf16[4096,1024]{1,0:T(8,128)(2,1)}) %all-gather.16.cloned.1.call-update) | async-done | bytes 8388624 | tf_op jit(solution)/shard_map/all_gather | solution.py:307
  583.8 12.0 fusion.6
  609.2 32.1 %all_to_all.64 = bf16[256,4,256]{2,0,1:T(8,128)(2,1)S(1)} all-to-all(bf16[256,4,256]{2,0,1:T(8,128)(2,1)S(1)} %bitcast.112), channel_id=1, replica_groups=mesh['dp'=8,'mp'=4] {'mp'}, dimensions={1} | all-to-all | bytes 1048576 | tf_op jit(solution)/shard_map/all_to_all | solution.py:190
  658.5 29.1 %all-to-all-done.3 = bf16[4,256,256]{2,1,0:T(8,128)(2,1)} async-done(((bf16[4,256,256]{2,1,0:T(8,128)(2,1)}), bf16[4,256,256]{2,1,0:T(8,128)(2,1)}, u32[]{:S(2)}, u32[]{:S(2)}) %all-to-all-start.3) | async-done | bytes 524320 | tf_op jit(solution)/shard_map/all_to_all | solution.py:195
  721.3 10.8 fusion.119
  733.6 9.5 fusion.27
  746.2 174.0 %reduce-scatter.9.cloned.1.call-done = f32[3,256,1024]{2,1,0:T(8,128)} async-done(((f32[3,1024,1024]{2,1,0:T(8,128)}), f32[3,256,1024]{2,1,0:T(8,128)}) %reduce-scatter.9.cloned.1.call-update) | async-done | bytes 3145744 | tf_op jit(solution)/shard_map/reduce_scatter | solution.py:320
  920.4 283.6 %reduce-scatter.17.cloned.1.call-done = f32[1024,1024]{1,0:T(8,128)} async-done(((f32[4096,1024]{1,0:T(8,128)}), f32[1024,1024]{1,0:T(8,128)}) %reduce-scatter.17.cloned.1.call-update) | async-done | bytes 4194320 | tf_op jit(solution)/shard_map/reduce_scatter | solution.py:320
  1204.3 283.2 %reduce-scatter.21.cloned.1.call-done = f32[1024,1024]{1,0:T(8,128)} async-done(((f32[4096,1024]{1,0:T(8,128)}), f32[1024,1024]{1,0:T(8,128)}) %reduce-scatter.21.cloned.1.call-update) | async-done | bytes 4194320 | tf_op jit(solution)/shard_map/reduce_scatter | solution.py:320
  1502.4 118.2 %all-reduce.6.cloned.1.call-done = f32[64,1024]{1,0:T(8,128)} async-done(((f32[64,1024]{1,0:T(8,128)}), f32[64,1024]{1,0:T(8,128)}) %all-reduce.6.cloned.1.call-update) | async-done | bytes 262160 | tf_op jit(solution)/shard_map/psum | solution.py:328
  1628.7 30.2 %reduce-scatter.15.cloned.1.call-done = f32[256,128]{1,0:T(8,128)} async-done(((f32[256,1024]{1,0:T(8,128)}), f32[256,128]{1,0:T(8,128)}) %reduce-scatter.15.cloned.1.call-update) | async-done | bytes 131088 | tf_op jit(solution)/shard_map/reduce_scatter | solution.py:321
  1660.4 47.7 %reduce-scatter.11.cloned.1.call-done = f32[3,256,128]{2,1,0:T(8,128)} async-done(((f32[3,256,1024]{2,1,0:T(8,128)}), f32[3,256,128]{2,1,0:T(8,128)}) %reduce-scatter.11.cloned.1.call-update) | async-done | bytes 393232 | tf_op jit(solution)/shard_map/reduce_scatter | solution.py:321
  1711.2 51.2 %reduce-scatter.19.cloned.1.call-done = f32[1024,128]{1,0:T(8,128)} async-done(((f32[1024,1024]{1,0:T(8,128)}), f32[1024,128]{1,0:T(8,128)}) %reduce-scatter.19.cloned.1.call-update) | async-done | bytes 524304 | tf_op jit(solution)/shard_map/reduce_scatter | solution.py:321
  1764.9 51.8 %reduce-scatter.23.cloned.1.call-done = f32[1024,128]{1,0:T(8,128)} async-done(((f32[1024,1024]{1,0:T(8,128)}), f32[1024,128]{1,0:T(8,128)}) %reduce-scatter.23.cloned.1.call-update) | async-done | bytes 524304 | tf_op jit(solution)/shard_map/reduce_scatter | solution.py:321
  1819.1 43.6 %all-reduce.7 = (f32[]{:T(128)}, f32[2,1024]{1,0:T(2,128)S(1)}, f32[3,3,1024]{2,1,0:T(4,128)S(1)}, f32[1024]{0:T(1024)S(1)}, f32[33,64]{1,0:T(8,128)S(1)}, /*index=5*/f32[2,64,64]{2,1,0:T(8,128)S(1)}) all-reduce(f32[]{:T(128)S(6)} %add.426, f32[2,1024]{1,0:T(2,128)S(1)} %pad_maximum_fusion.13, ...), channel_id=1, replica_groups=mesh['dp'=8,'mp'=4] {'dp','mp'}, use_global_device_ids=true, to_apply=%region_20.21 | all-reduce | flops 22593 | bytes 180744 | tf_op jit(solution)/shard_map/psum | solution.py:329
  (350 shorter events, 204.4 us)
Async XLA Ops:
  7.2 31.8 %all-gather.8.cloned.1.call-start = ((), (), s32[]{:S(2)}) async-start(), calls=%async_computation.12 | async-start | bytes 1769472 | tf_op jit(solution)/shard_map/all_gather | solution.py:306
  9.0 60.6 %all-gather.18.cloned.1.call-start = ((), (), s32[]{:S(2)}) async-start(), calls=%async_computation.17 | async-start | bytes 2359296 | tf_op jit(solution)/shard_map/all_gather | solution.py:306
  10.9 89.3 %all-gather.14.cloned.1.call-start = ((), (), s32[]{:S(2)}) async-start(), calls=%async_computation.15 | async-start | bytes 2359296 | tf_op jit(solution)/shard_map/all_gather | solution.py:306
  12.8 204.2 %all-gather.10.cloned.1.call-start = ((), (), s32[]{:S(2)}) async-start(), calls=%async_computation.13 | async-start | bytes 7864320 | tf_op jit(solution)/shard_map/all_gather | solution.py:307
  39.1 290.9 %all-gather.12.cloned.1.call-start = ((), (), s32[]{:S(2)}) async-start(), calls=%async_computation.14 | async-start | bytes 2621440 | tf_op jit(solution)/shard_map/all_gather | solution.py:307
  50.1 384.4 %all-gather.20.cloned.1.call-start = ((), (), s32[]{:S(2)}) async-start(), calls=%async_computation.18 | async-start | bytes 10485760 | tf_op jit(solution)/shard_map/all_gather | solution.py:307
  69.6 514.2 %all-gather.16.cloned.1.call-start = ((), (), s32[]{:S(2)}) async-start(), calls=%async_computation.16 | async-start | bytes 10485760 | tf_op jit(solution)/shard_map/all_gather | solution.py:307
  100.2 22.5 %collective-permute-start = (bf16[16,1024]{1,0:T(8,128)(2,1)S(1)}, bf16[16,1024]{1,0:T(8,128)(2,1)S(1)}, u32[]{:S(2)}, u32[]{:S(2)}) collective-permute-start(bf16[16,1024]{1,0:T(8,128)(2,1)S(1)} %slice.90), channel_id=1, source_target_pairs={{0,1},{1,2},{2,3},{4,5},{5,6},{6,7},{8,9},{9,10},{10,11},{12,13},{... | collective-permute-start | bytes 98312 | tf_op jit(solution)/shard_map/ppermute | solution.py:146
  227.4 34.1 %all-to-all-start = ((bf16[256,4,256]{2,0,1:T(8,128)(2,1)}), bf16[256,4,256]{2,0,1:T(8,128)(2,1)}, u32[]{:S(2)}, u32[]{:S(2)}) async-start(bf16[256,4,256]{2,0,1:T(8,128)(2,1)} %bitcast.111), calls=%async_computation | async-start | bytes 1048576 | tf_op jit(solution)/shard_map/all_to_all | solution.py:190
  288.3 36.9 %all-to-all-start.1 = ((bf16[4,256,256]{2,1,0:T(8,128)(2,1)}), bf16[4,256,256]{2,1,0:T(8,128)(2,1)}, u32[]{:S(2)}, u32[]{:S(2)}) async-start(bf16[4,256,256]{2,1,0:T(8,128)(2,1)} %bitcast.115), calls=%async_computation.1 | async-start | bytes 1048576 | tf_op jit(solution)/shard_map/all_to_all | solution.py:195
  292.6 452.9 %reduce-scatter.13.cloned.1.call-start = ((), (), s32[]{:S(2)}) async-start(), calls=%async_computation.21 | async-start | bytes 5242880 | tf_op jit(solution)/shard_map/reduce_scatter | solution.py:320
  653.6 34.0 %all-to-all-start.3 = ((bf16[4,256,256]{2,1,0:T(8,128)(2,1)}), bf16[4,256,256]{2,1,0:T(8,128)(2,1)}, u32[]{:S(2)}, u32[]{:S(2)}) async-start(bf16[4,256,256]{2,1,0:T(8,128)(2,1)} %bitcast.114), calls=%async_computation.3 | async-start | bytes 1048576 | tf_op jit(solution)/shard_map/all_to_all | solution.py:195
  657.7 262.6 %reduce-scatter.9.cloned.1.call-start = ((), (), s32[]{:S(2)}) async-start(), calls=%async_computation.19 | async-start | bytes 15728640 | tf_op jit(solution)/shard_map/reduce_scatter | solution.py:320
  691.7 6.7 collective-permute-start.1
  709.4 494.6 %reduce-scatter.17.cloned.1.call-start = ((), (), s32[]{:S(2)}) async-start(), calls=%async_computation.23 | async-start | bytes 20971520 | tf_op jit(solution)/shard_map/reduce_scatter | solution.py:320
  720.3 767.2 %reduce-scatter.21.cloned.1.call-start = ((), (), s32[]{:S(2)}) async-start(), calls=%async_computation.25 | async-start | bytes 20971520 | tf_op jit(solution)/shard_map/reduce_scatter | solution.py:320
  732.1 888.5 %all-reduce.6.cloned.1.call-start = ((), (), s32[]{:S(2)}) async-start(), calls=%async_computation.27 | async-start | bytes 524288 | tf_op jit(solution)/shard_map/psum | solution.py:328
  745.4 913.4 %reduce-scatter.15.cloned.1.call-start = ((), (), s32[]{:S(2)}) async-start(), calls=%async_computation.22 | async-start | bytes 1179648 | tf_op jit(solution)/shard_map/reduce_scatter | solution.py:321
  746.2 961.9 %reduce-scatter.11.cloned.1.call-start = ((), (), s32[]{:S(2)}) async-start(), calls=%async_computation.20 | async-start | bytes 3538944 | tf_op jit(solution)/shard_map/reduce_scatter | solution.py:321
  920.3 842.1 %reduce-scatter.19.cloned.1.call-start = ((), (), s32[]{:S(2)}) async-start(), calls=%async_computation.24 | async-start | bytes 4718592 | tf_op jit(solution)/shard_map/reduce_scatter | solution.py:321
  1204.0 283.5 %copy-start.90 = (f32[272]{0:T(512)S(1)}, f32[272]{0:T(512)}, u32[]{:S(2)}) copy-start(f32[272]{0:T(512)} %copy-done.89) | copy-start | bytes 3268
  1204.0 612.6 %reduce-scatter.23.cloned.1.call-start = ((), (), s32[]{:S(2)}) async-start(), calls=%async_computation.26 | async-start | bytes 4718592 | tf_op jit(solution)/shard_map/reduce_scatter | solution.py:321
  1628.7 254.3 %copy-start.40 = (f32[1024,128]{1,0:T(8,128)S(1)}, f32[1024,128]{1,0:T(8,128)}, u32[]{:S(2)}) copy-start(f32[1024,128]{1,0:T(8,128)} %param.62) | copy-start | bytes 1572868
  1628.7 254.3 %copy-start.59 = (f32[1024,128]{1,0:T(8,128)S(1)}, f32[1024,128]{1,0:T(8,128)}, u32[]{:S(2)}) copy-start(f32[1024,128]{1,0:T(8,128)} %param.63) | copy-start | bytes 1572868
  (100 other events, 3971.7 us)
Sparse Core Ops, SparseCore 0:
  10.5 28.4 all-gather.7
  41.5 28.0 all-gather.17
  72.1 28.0 all-gather.13
  101.6 115.3 all-gather.9
  218.4 55.0 all-gather.11
  274.9 159.4 all-gather.19
  436.0 147.7 all-gather.15
  603.4 91.8 reduce-scatter.12
  709.5 210.7 reduce-scatter.8
  922.5 281.4 reduce-scatter.16
  1206.4 281.0 reduce-scatter.20
  1493.4 127.1 all-reduce.5
  1623.8 34.9 reduce-scatter.14
  1662.0 46.0 reduce-scatter.10
  1711.3 51.0 reduce-scatter.18
  1765.6 51.0 reduce-scatter.22

commit v2 on v1

--- a/solution.py
+++ b/solution.py
@@ -330,7 +330,435 @@
         return tuple(small) + large, total
 
 
+class Place:
+    def __init__(self, n_mp):
+        dp = lax.axis_index("dp")
+        self.n_mp = n_mp
+        self.dp = dp
+        self.z = lax.axis_index("mp")
+        self.y, self.x, self.c = dp // 4, (dp // 2) % 2, dp % 2
+        self.by_x = (dp + 2 - 4 * self.x, self.z)
+        self.by_y = (dp + 4 - 8 * self.y, self.z)
+        self.by_core = (dp + 1 - 2 * self.c, self.z)
+
+    def up(self, off):
+        return lax.rem(self.z + off, self.n_mp)
+
+    def by_z(self, off):
+        return (self.dp, self.up(off))
+
+    def column(self, y, x, c):
+        return pl.ds(pl.multiple_of((4 * y + 2 * x + c) * LANES, LANES), LANES)
+
+
+def greet(here):
+    barrier = pltpu.get_barrier_semaphore()
+    peers = [here.by_x, here.by_y, here.by_core]
+    peers += [here.by_z(off) for off in range(1, here.n_mp)]
+    for peer in peers:
+        pl.semaphore_signal(barrier, inc=1, device_id=peer, device_id_type=MESH_IDS)
+    pl.semaphore_wait(barrier, len(peers))
+
+
+def push(source, target, sems, index, peer):
+    copy = pltpu.make_async_remote_copy(
+        src_ref=source,
+        dst_ref=target,
+        send_sem=sems[0].at[index],
+        recv_sem=sems[1].at[index],
+        device_id=peer,
+        device_id_type=MESH_IDS,
+    )
+    copy.start()
+    return copy
+
+
+GATHER_COPIES = 39
+
+
+def gather_kernel(n_mp, count, *refs):
+    shards, wholes = refs[:count], refs[count : 2 * count]
+    send, recv, local = refs[2 * count :]
+    here = Place(n_mp)
+    greet(here)
+
+    def block(w, z, y, x, c, half=None):
+        whole = wholes[w]
+        depth = shards[w].shape[-2]
+        start, size = z * depth, depth
+        if half is not None:
+            size = depth // 2
+            start = start + half * size
+        spot = (pl.ds(pl.multiple_of(start, 16), size), here.column(y, x, c))
+        return whole.at[(slice(None),) + spot] if len(whole.shape) == 3 else whole.at[spot]
+
+    y, x, c = here.y, here.x, here.c
+    other_y, other_x, other_c = 1 - y, 1 - x, 1 - c
+    started = []
+    kept = []
+    step = [0] * count
+
+    def relay(w, source, spot, peer):
+        index = step[w]
+        step[w] += 1
+        copy = push(source, spot, (send.at[w], recv.at[w]), index, peer)
+        started.append(copy)
+        return copy
+
+    own, by_z, by_x, by_y = {}, {}, {}, {}
+    for w in range(count):
+        mine = block(w, here.z, y, x, c)
+        keep = pltpu.make_async_copy(shards[w], mine, local.at[w])
+        keep.start()
+        kept.append(keep)
+        by_z[w] = [relay(w, shards[w], mine, here.by_z(off)) for off in range(1, n_mp)]
+        by_x[w] = [relay(w, shards[w], mine, here.by_x)]
+        by_y[w] = [relay(w, shards[w], mine, here.by_y)]
+        relay(w, shards[w], mine, here.by_core)
+    for w in range(count):
+        for off in range(1, n_mp):
+            by_z[w][off - 1].wait_recv()
+            z = here.up(n_mp - off)
+            got = block(w, z, y, x, c)
+            by_x[w].append(relay(w, got, got, here.by_x))
+            by_y[w].append(relay(w, got, got, here.by_y))
+            relay(w, got, got, here.by_core)
+        far = []
+        for off in range(n_mp):
+            z = here.up(n_mp - off) if off else here.z
+            by_x[w][off].wait_recv()
+            got = block(w, z, y, other_x, c, 1)
+            far.append((relay(w, got, got, here.by_y), z, 1))
+            got = block(w, z, y, other_x, c)
+            relay(w, got, got, here.by_core)
+            by_y[w][off].wait_recv()
+            got = block(w, z, other_y, x, c, 0)
+            far.append((relay(w, got, got, here.by_x), z, 0))
+            got = block(w, z, other_y, x, c)
+            relay(w, got, got, here.by_core)
+        own[w] = far
+    for w in range(count):
+        for copy, z, half in own[w]:
+            copy.wait_recv()
+            got = block(w, z, other_y, other_x, c, half)
+            relay(w, got, got, here.by_core)
+    for keep in kept:
+        keep.wait()
+    waited = set()
+    for w in range(count):
+        for copy in by_z[w] + by_x[w] + by_y[w] + [f[0] for f in own[w]]:
+            waited.add(id(copy))
+    for copy in started:
+        if id(copy) not in waited:
+            copy.wait_recv()
+        copy.wait_send()
+
+
+def gather_call(shards, n_mp, collective_id):
+    count = len(shards)
+    wholes = [
+        jax.ShapeDtypeStruct(s.shape[:-2] + (s.shape[-2] * n_mp, s.shape[-1] * 8), BF)
+        for s in shards
+    ]
+    copies = n_mp - 1 + 3 + 3 * (n_mp - 1) + 4 * n_mp + 2 * n_mp
+    moved = 2 * sum(math.prod(s.shape) for s in wholes)
+    return pl.pallas_call(
+        functools.partial(gather_kernel, n_mp, count),
+        out_shape=wholes,
+        in_specs=[pl.BlockSpec(memory_space=pltpu.VMEM)] * count,
+        out_specs=[pl.BlockSpec(memory_space=pl.ANY)] * count,
+        scratch_shapes=[
+            pltpu.SemaphoreType.DMA((count, copies)),
+            pltpu.SemaphoreType.DMA((count, copies)),
+            pltpu.SemaphoreType.DMA((count,)),
+        ],
+        compiler_params=pltpu.CompilerParams(
+            collective_id=collective_id, has_side_effects=True, vmem_limit_bytes=16 << 20
+        ),
+        cost_estimate=pl.CostEstimate(flops=0, bytes_accessed=8 * moved, transcendentals=0),
+        name=f"gather_{collective_id}",
+    )(*shards)
+
+
+def added(target, terms, rows):
+    piece = min(rows, 128)
+
+    def body(i, carry):
+        at = pl.ds(pl.multiple_of(i * piece, piece), piece)
+        total = terms[0][at, :].astype(F32)
+        for term in terms[1:]:
+            total = total + term[at, :].astype(F32)
+        target[at, :] = total.astype(target.dtype)
+        return carry
+
+    lax.fori_loop(0, rows // piece, body, 0)
+
+
+def reduce_kernel(n_mp, plan, *refs):
+    count = len(plan)
+    grads, sums = refs[:count], refs[count : 2 * count]
+    rest = refs[2 * count :]
+    buffers = [rest[8 * w : 8 * w + 8] for w in range(count)]
+    send, recv, local = rest[8 * count :]
+    here = Place(n_mp)
+    greet(here)
+    y, x, c = here.y, here.x, here.c
+    half_wide = 4 * LANES
+    mine = pl.ds(pl.multiple_of(c * half_wide, half_wide), half_wide)
+    theirs = pl.ds(pl.multiple_of((1 - c) * half_wide, half_wide), half_wide)
+    offs = [*range(1, n_mp), 0]
+    chunks = []
+    base = 0
+    for w, depth in enumerate(plan):
+        size = depth // 2
+        for turn, off in enumerate(offs):
+            for half in range(2):
+                chunks.append((w, turn, off, half, size, base))
+                base += 4
+    copies = {}
+
+    def stage_zero(q):
+        w, turn, off, half, size, base = chunks[q]
+        own, core_in = buffers[w][:2]
+        at = 2 * turn + half
+        start = here.up(off) * plan[w] + half * size
+        row = pl.ds(pl.multiple_of(start, 8), size)
+        sent = push(grads[w].at[row, theirs], core_in.at[at], (send, recv), base, here.by_core)
+        kept = pltpu.make_async_copy(grads[w].at[row, mine], own.at[at], local.at[q])
+        kept.start()
+        copies[q, 0] = (sent, kept)
+
+    def stage_one(q):
+        w, turn, off, half, size, base = chunks[q]
+        own, core_in, pair, pair_in = buffers[w][:4]
+        at = 2 * turn + half
+        sent, kept = copies[q, 0]
+        kept.wait()
+        sent.wait_recv()
+        for by in range(2):
+            for bx in range(2):
+                spot = pl.ds((2 * by + bx) * LANES, LANES)
+                near, far = (bx, by) if half == 0 else (by, bx)
+                added(
+                    pair.at[at, near, far],
+                    [own.at[at, :, spot], core_in.at[at, :, spot]],
+                    size,
+                )
+        away = 1 - x if half == 0 else 1 - y
+        peer = here.by_x if half == 0 else here.by_y
+        copies[q, 1] = push(pair.at[at, away], pair_in.at[at], (send, recv), base + 1, peer)
+
+    def stage_two(q):
+        w, turn, off, half, size, base = chunks[q]
+        pair, pair_in, quad, quad_in = buffers[w][2:6]
+        at = 2 * turn + half
+        copies[q, 1].wait_recv()
+        me = x if half == 0 else y
+        for far in range(2):
+            added(quad.at[at, far], [pair.at[at, me, far], pair_in.at[at, far]], size)
+        away = 1 - y if half == 0 else 1 - x
+        peer = here.by_y if half == 0 else here.by_x
+        copies[q, 2] = push(quad.at[at, away], quad_in.at[at], (send, recv), base + 2, peer)
+
+    def stage_three(q):
+        w, turn, off, half, size, base = chunks[q]
+        quad, quad_in, plane, plane_in = buffers[w][4:8]
+        at = 2 * turn + half
+        copies[q, 2].wait_recv()
+        me = y if half == 0 else x
+        added(plane.at[at], [quad.at[at, me], quad_in.at[at]], size)
+        if off:
+            copies[q, 3] = push(
+                plane.at[at], plane_in.at[at], (send, recv), base + 3, here.by_z(off)
+            )
+
+    def stage_four(q):
+        w, turn, off, half, size, base = chunks[q]
+        plane, plane_in = buffers[w][6:8]
+        first = q - 2 * (n_mp - 1)
+        for k in range(n_mp - 1):
+            copies[first + 2 * k, 3].wait_recv()
+        terms = [plane_in.at[2 * k + half] for k in range(n_mp - 1)]
+        added(
+            sums[w].at[pl.ds(half * size, size)],
+            [plane.at[2 * turn + half]] + terms,
+            size,
+        )
+
+    total = len(chunks)
+    for q in range(total):
+        stage_zero(q)
+    for q in range(total + 6):
+        if q < total:
+            stage_one(q)
+        if 0 <= q - 2 < total:
+            stage_two(q - 2)
+        if 0 <= q - 4 < total:
+            stage_three(q - 4)
+    for q in range(total):
+        if chunks[q][2] == 0:
+            stage_four(q)
+    for (q, stage), copy in copies.items():
+        (copy[0] if stage == 0 else copy).wait_send()
+
+
+def reduce_call(grads, n_mp, collective_id):
+    plan = [g.shape[0] // n_mp for g in grads]
+    scratch = []
+    for g, depth in zip(grads, plan):
+        n, size, dt = 2 * n_mp, depth // 2, g.dtype
+        scratch += [
+            pltpu.VMEM((n, size, 4 * LANES), dt),
+            pltpu.VMEM((n, size, 4 * LANES), dt),
+            pltpu.VMEM((n, 2, 2, size, LANES), dt),
+            pltpu.VMEM((n, 2, size, LANES), dt),
+            pltpu.VMEM((n, 2, size, LANES), dt),
+            pltpu.VMEM((n, size, LANES), dt),
+            pltpu.VMEM((n, size, LANES), dt),
+            pltpu.VMEM((n - 2, size, LANES), dt),
+        ]
+    chunks = 2 * n_mp * len(grads)
+    moved = sum(g.size * g.dtype.itemsize for g in grads)
+    return pl.pallas_call(
+        functools.partial(reduce_kernel, n_mp, plan),
+        out_shape=[jax.ShapeDtypeStruct((depth, LANES), F32) for depth in plan],
+        in_specs=[pl.BlockSpec(memory_space=pl.ANY)] * len(grads),
+        out_specs=[pl.BlockSpec(memory_space=pltpu.VMEM)] * len(grads),
+        scratch_shapes=scratch
+        + [
+            pltpu.SemaphoreType.DMA((4 * chunks,)),
+            pltpu.SemaphoreType.DMA((4 * chunks,)),
+            pltpu.SemaphoreType.DMA((chunks,)),
+        ],
+        compiler_params=pltpu.CompilerParams(
+            collective_id=collective_id, has_side_effects=True, vmem_limit_bytes=58 << 20
+        ),
+        cost_estimate=pl.CostEstimate(flops=0, bytes_accessed=8 * moved, transcendentals=0),
+        name=f"reduce_{collective_id}",
+    )(*grads)
+
+
+def spread_kernel(n_mp, part_ref, whole_ref, send, recv, local):
+    here = Place(n_mp)
+    greet(here)
+    y, x, c = here.y, here.x, here.c
+    own = pltpu.make_async_copy(part_ref, whole_ref.at[y, x, c, here.z], local)
+    own.start()
+    sems = (send, recv)
+    sent = [
+        push(part_ref, whole_ref.at[y, x, c, here.z], sems, off - 1, here.by_z(off))
+        for off in range(1, n_mp)
+    ]
+    own.wait()
+    for copy in sent:
+        copy.wait_recv()
+    line = whole_ref.at[y, x, c]
+    sent.append(push(line, line, sems, n_mp - 1, here.by_x))
+    sent.append(push(line, line, sems, n_mp, here.by_core))
+    sent[-2].wait_recv()
+    sent[-1].wait_recv()
+    for spot in ((y, x, c), (y, 1 - x, c)):
+        line = whole_ref.at[spot]
+        sent.append(push(line, line, sems, len(sent), here.by_y))
+    line = whole_ref.at[y, 1 - x, c]
+    sent.append(push(line, line, sems, len(sent), here.by_core))
+    sent[-3].wait_recv()
+    sent[-2].wait_recv()
+    first = len(sent)
+    for bx in range(2):
+        line = whole_ref.at[1 - y, bx, c]
+        sent.append(push(line, line, sems, len(sent), here.by_core))
+    for copy in sent[first - 1 :]:
+        copy.wait_recv()
+    for copy in sent:
+        copy.wait_send()
+
+
+def spread_call(part, n_mp, collective_id):
+    copies = n_mp + 6
+    return pl.pallas_call(
+        functools.partial(spread_kernel, n_mp),
+        out_shape=jax.ShapeDtypeStruct((2, 2, 2, n_mp) + part.shape, F32),
+        in_specs=[pl.BlockSpec(memory_space=pltpu.VMEM)],
+        out_specs=pl.BlockSpec(memory_space=pltpu.VMEM),
+        scratch_shapes=[
+            pltpu.SemaphoreType.DMA((copies,)),
+            pltpu.SemaphoreType.DMA((copies,)),
+            pltpu.SemaphoreType.DMA,
+        ],
+        compiler_params=pltpu.CompilerParams(
+            collective_id=collective_id, has_side_effects=True
+        ),
+        name=f"spread_{collective_id}",
+    )(part)
+
+
+def by_core_first(values):
+    split = values.reshape(values.shape[0], 4, 2, -1)
+    return split.transpose(0, 2, 1, 3).reshape(values.shape)
+
+
+def packed(small, group):
+    flat = jnp.concatenate([s.reshape(-1) for s in small])
+    wide = 8 * LANES
+    count = -(-flat.size // (wide * group)) * group
+    return jnp.pad(flat, (0, count * wide - flat.size)).reshape(count, wide)
+
+
+def unpacked(matrix, like):
+    flat, parts, at = matrix.reshape(-1), [], 0
+    for s in like:
+        parts.append(flat[at : at + s.size].reshape(s.shape))
+        at += s.size
+    return tuple(parts)
+
+
+class KernelPaths:
+    def __init__(self, n_mp):
+        self.n_mp = n_mp
+
+    def gather_mixer(self, in_shard, out_shard):
+        return gather_call([in_shard, out_shard], self.n_mp, 1)
+
+    def gather_ffn(self, up_shard, down_shard):
+        return gather_call([up_shard, down_shard], self.n_mp, 2)
+
+    def partial_grad(self, left, right, parts):
+        if parts:
+            left = left.reshape(left.shape[0], parts, self.n_mp, -1)
+            left = left.transpose(0, 2, 1, 3).reshape(left.shape[0], -1)
+        return lax.dot_general(
+            left, by_core_first(right), COLS_COLS, preferred_element_type=F32
+        ).astype(BF)
+
+    def reduce_ffn(self, up_pair, down_pair):
+        pair = [self.partial_grad(*up_pair), self.partial_grad(*down_pair)]
+        return tuple(reduce_call(pair, self.n_mp, 3))
+
+    def reduce_mixer(self, in_pair, out_pair, small, ffn_sums):
+        matrix = packed(small, 16 * self.n_mp)
+        grads = [
+            self.partial_grad(*in_pair),
+            self.partial_grad(*out_pair),
+            by_core_first(matrix),
+        ]
+        in_sum, out_sum, small_part = reduce_call(grads, self.n_mp, 4)
+        large = (in_sum, out_sum) + tuple(ffn_sums)
+        mark = jnp.full((8, LANES), squares(large))
+        part = jnp.concatenate([small_part, mark], axis=0)
+        whole = spread_call(part, self.n_mp, 5)
+        depth = small_part.shape[0]
+        total_large = jnp.sum(whole[..., depth, 0])
+        matrix = whole[..., :depth, :].transpose(3, 4, 0, 1, 2, 5).reshape(matrix.shape)
+        sums = unpacked(matrix, small)
+        depth = in_sum.shape[0] // in_pair[2]
+        in_sum = in_sum.reshape(in_pair[2], depth, LANES)
+        return sums + (in_sum,) + large[1:], total_large + squares(sums)
+
+
 def choose_paths(mesh):
+    if mesh.shape["dp"] == 8 and mesh.shape["mp"] == 4:
+        return KernelPaths(mesh.shape["mp"])
     return PlainPaths()
 
 

time: 1900 us -> 602 us (0.32)
  waiting for transfers between devices: 1530 us -> 9.16 us
  Pallas kernels: 0 us -> 297 us
  blocking collectives: 86.5 us -> 0 us
  local copies, waits for them, and re-layouts: 21.3 us -> 56.8 us
  matrix products: 142 us -> 121 us
    reduce_scatter x8 -> x0, waiting for transfers between devices: 922 us -> none  [the longest x4 741 us: reduced(): part = lax.psum_scatter(grad, 'mp', scatter_dimension=along - 1, tiled=True)]
    all_gather x7 -> x0, waiting for transfers between devices: 410 us -> none  [the longest x4 333 us: gather(): return lax.all_gather(part, 'mp', axis=along - 1, tiled=True)]
    pallas_call x0 -> x5, Pallas kernels: none -> 297 us  [the longest x2 142 us: reduce_call(): pl.pallas_call(functools.partial(reduce_kernel, n_mp, plan), out_shape=[j...]
    psum x1 -> x0, waiting for transfers between devices: 118 us -> none  [reduce_mixer(): small = lax.psum(small, ('dp', 'mp'))]
    all_to_all x2, waiting for transfers between devices: 59.5 us -> 0.01 us  [to_tokens(): lax.all_to_all(values.astype(BF), 'mp', split_axis=0, concat_axis=1, tile...]
    psum x1 -> x0, blocking collectives: 43.6 us -> none  [reduce_mixer(): total = lax.psum(squares(large), ('dp', 'mp')) + squares(small)]
    all_to_all x1 -> x0, blocking collectives: 32.1 us -> none  [to_channels(): lax.all_to_all(values.astype(BF), 'mp', split_axis=1, concat_axis=0, tile...]
  transfers between devices with their start and end apart: 21 -> 6, of which waited for: 18 -> 2; matrix products, arithmetic and copies ran while one was open for 9% -> 15% of each run, Pallas kernels for 0% -> 37%
where the time goes in v2:
time: 602 us; the launch traced here: 595 us
  Pallas kernels  297 us (49%)
  matrix products  121 us (20%)
  other arithmetic  66.6 us (11%)
  local copies, waits for them, and re-layouts  56.8 us (9%)
  starting transfers between devices  32 us (5%)
  between operations  11.5 us (2%)
  waiting for transfers between devices  9.16 us (2%)
    pallas_call x2, Pallas kernels, reduce_call(): pl.pallas_call(functools.partial(reduce_kernel, n_mp, plan), out_shape=[j...  142 us
    pallas_call x2, Pallas kernels, gather_call(): pl.pallas_call(functools.partial(gather_kernel, n_mp, count), out_shape=w...  139 us
    dot_general x3, matrix products, signal_of(): lax.dot_general(table, both, COLS_COLS, precision=HIGH, preferred_element...  25.3 us
    unnamed x205, local copies, waits for them, and re-layouts  22.5 us
    dot_general x11, matrix products, dense(): return jnp.dot(a, b, precision=HIGHEST, preferred_element_type=F32)  22.1 us
    dot_general x4, matrix products, partial_grad(): lax.dot_general(left, by_core_first(right), COLS_COLS, preferred_element_...  19.3 us
    all_to_all x2, starting transfers between devices, to_channels(): lax.all_to_all(values.astype(BF), 'mp', split_axis=1, concat_axis=0, tile...  17.3 us
    dot_general x3, matrix products, spectrum(): both = jnp.dot(table, signal, precision=HIGH, preferred_element_type=F32)  17.1 us
  transfers between devices with their start and end apart: 6, of which 2 were waited for; matrix products, arithmetic and copies ran while one was open for 15% of the time, Pallas kernels for 37%

profile of v2, /device:TPU:0, one launch (start us, length us, event | category | flops | bytes accessed | tf_op | source)
XLA Modules:
  0.0 594.6 jit_solution(8363426891150618637)
XLA Ops:
  2.2 4.9 collective-permute-start
  22.5 4.9 fusion.58
  28.2 47.6 %gather_1.1 = (bf16[3,1024,1024]{2,1,0:T(8,128)(2,1)S(1)}, bf16[1024,1024]{1,0:T(8,128)(2,1)S(1)}) custom-call(bf16[3,256,128]{2,1,0:T(8,128)(2,1)S(1)} %convert_element_type.120.refs_0_, bf16[256,128]{1,0:T(8,128)(2,1)S(1)} %convert_element_type.121.refs_1_), custom_call_target="tpu_custom_call" | custom-call | bytes 67108864 | tf_op jit(solution)/shard_map/gather_1/pallas_call | solution.py:465
  84.8 8.5 %all-to-all-start = ((bf16[256,4,256]{2,0,1:T(8,128)(2,1)}), bf16[256,4,256]{2,0,1:T(8,128)(2,1)S(1)}, u32[]{:S(2)}, u32[]{:S(2)}) async-start(bf16[256,4,256]{2,0,1:T(8,128)(2,1)} %bitcast.126), calls=%async_computation | async-start | bytes 1048576 | tf_op jit(solution)/shard_map/all_to_all | solution.py:190
  97.8 4.9 fusion.44
  102.7 5.5 all-to-all-done
  108.2 6.1 %fusion.45 = f32[2048,256]{1,0:T(8,128)S(1)} fusion(bf16[1024,256]{1,0:T(8,128)(2,1)S(1)} %bitcast.165, f32[1024,1024]{1,0:T(8,128)} %bitcast.141, f32[1024,1024]{1,0:T(8,128)} %bitcast.135), kind=kOutput, calls=%fused_computation.92 | convolution fusion | flops 3223322624 | bytes 11010048 | tf_op jit(solution)/shard_map/dot_general | solution.py:180
  117.2 8.0 %fusion.37 = bf16[1024,256]{1,0:T(8,128)(2,1)} fusion(f32[1024,256]{1,0:T(8,128)S(1)} %get-tuple-element.113, f32[1024,256]{1,0:T(8,128)S(1)} %get-tuple-element.112, f32[1024,1024]{1,0:T(8,128)S(1)} %bitcast.144, f32[1024,1024]{1,0:T(8,128)S(1)} %bitcast.138, f32[]{:T(128)S(6)} %div.217), kind=kOutput, calls=%fused_computation.52 | convolution fusion | flops 3224371200 | bytes 11010052 | tf_op jit(solution)/shard_map/dot_general | solution.py:185
  132.7 91.8 %gather_2.1 = (bf16[4096,1024]{1,0:T(8,128)(2,1)S(1)}, bf16[4096,1024]{1,0:T(8,128)(2,1)S(1)}) custom-call(bf16[1024,128]{1,0:T(8,128)(2,1)S(1)} %convert_element_type.131.refs_0_, bf16[1024,128]{1,0:T(8,128)(2,1)S(1)} %convert_element_type.132.refs_1_), custom_call_target="tpu_custom_call" | custom-call | bytes 134217728 | tf_op jit(solution)/shard_map/gather_2/pallas_call | solution.py:465
  244.5 8.0 %fusion.130 = f32[256,4096]{1,0:T(8,128)} fusion(bf16[256,1024]{1,0:T(8,128)(2,1)S(1)} %multiply_convert_fusion.2, bf16[4096,1024]{1,0:T(8,128)(2,1)} %copy-done.1), kind=kOutput, calls=%fused_computation.266 | convolution fusion | flops 2147483648 | bytes 13107200 | tf_op jit(solution)/shard_map/dot_general | solution.py:213
  252.6 6.8 %fusion.6 = bf16[256,4096]{1,0:T(8,128)(2,1)S(1)} fusion(f32[256,4096]{1,0:T(8,128)} %fusion.130, bf16[4096,1024]{1,0:T(8,128)(2,1)S(1)} %bitcast.129, bf16[256,1024]{1,0:T(8,128)(2,1)S(1)} %copy-done.49), kind=kOutput, calls=%fused_computation.13 | convolution fusion | flops 2168455168 | bytes 15204352 | tf_op jit(solution)/shard_map/dot_general | solution.py:219
  272.5 8.7 %all-to-all-start.2 = ((bf16[256,4,256]{2,0,1:T(8,128)(2,1)}), bf16[256,4,256]{2,0,1:T(8,128)(2,1)}, u32[]{:S(2)}, u32[]{:S(2)}) async-start(bf16[256,4,256]{2,0,1:T(8,128)(2,1)} %bitcast.125), calls=%async_computation.2 | async-start | bytes 1048576 | tf_op jit(solution)/shard_map/all_to_all | solution.py:190
  284.4 7.4 %convolution_convert_fusion.1.refs_0_ = bf16[4096,1024]{1,0:T(8,128)(2,1)} fusion(bf16[256,4096]{1,0:T(8,128)(2,1)} %copy-done.36, bf16[256,1024]{0,1:T(8,128)(2,1)S(1)} %bitcast.160), kind=kOutput, calls=%fused_computation.2 | convolution fusion | flops 2151677952 | bytes 11010048 | tf_op jit(solution)/shard_map/dot_general | solution.py:730
  291.9 5.3 convolution_convert_fusion.refs_1_
  297.2 83.0 %reduce_3.1 = (f32[1024,128]{1,0:T(8,128)}, f32[1024,128]{1,0:T(8,128)}) custom-call(bf16[4096,1024]{1,0:T(8,128)(2,1)} %convolution_convert_fusion.1.refs_0_, bf16[4096,1024]{1,0:T(8,128)(2,1)} %convolution_convert_fusion.refs_1_), custom_call_target="tpu_custom_call" | custom-call | bytes 134217728 | tf_op jit(solution)/shard_map/reduce_3/pallas_call | solution.py:622
  383.7 6.9 %fusion.36 = bf16[256,1024]{1,0:T(8,128)(2,1)} fusion(f32[256,1024]{1,0:T(8,128)S(1)} %get-tuple-element.103, bf16[4096,1024]{1,0:T(8,128)(2,1)} %copy-done, f32[256,4096]{1,0:T(8,128)S(1)} %copy-done.96), kind=kOutput, calls=%fused_computation.51 | convolution fusion | flops 2157445120 | bytes 14155776 | tf_op jit(solution)/shard_map/dot_general | solution.py:217
  390.6 6.1 %fusion.43 = f32[2048,256]{1,0:T(8,128)S(1)} fusion(bf16[1024,256]{1,0:T(8,128)(2,1)} %bitcast.17, f32[1024,1024]{1,0:T(8,128)} %bitcast.142, f32[1024,1024]{1,0:T(8,128)} %bitcast.136), kind=kOutput, calls=%fused_computation.90 | convolution fusion | flops 3223322624 | bytes 11010048 | tf_op jit(solution)/shard_map/dot_general | solution.py:180
  400.3 7.9 %fusion.40 = bf16[1024,256]{1,0:T(8,128)(2,1)} fusion(f32[1024,256]{1,0:T(8,128)S(1)} %get-tuple-element.115, f32[1024,256]{1,0:T(8,128)S(1)} %get-tuple-element.116, f32[1024,1024]{1,0:T(8,128)S(1)} %bitcast.145, f32[1024,1024]{1,0:T(8,128)S(1)} %bitcast.139, f32[]{:T(128)S(6)} %div.217), kind=kOutput, calls=%fused_computation.53 | convolution fusion | flops 3224371200 | bytes 11010052 | tf_op jit(solution)/shard_map/dot_general | solution.py:185
  412.4 9.4 %fusion.27 = f32[1024,256]{1,0:T(8,128)S(1)} fusion(f32[1024,256]{1,0:T(8,128)S(1)} %get-tuple-element.109, f32[1024,256]{1,0:T(8,128)S(1)} %get-tuple-element.108, f32[1024,1024]{1,0:T(8,128)} %bitcast.143, f32[1024,1024]{1,0:T(8,128)} %bitcast.137, f32[1024]{0:T(1024)} %copy-done.85, f32[256]{0:T(256)} %copy-done.94, f32[]{:T(128)S(6)} %div.217), kind=kOutput, calls=%fused_computation.46 | convolution fusion | flops 3224633344 | bytes 11539460 | tf_op jit(solution)/shard_map/dot_general | solution.py:185
  449.6 6.2 %multiply_reduce_fusion.2 = (f32[3072]{0:T(1024)S(1)}, f32[3072]{0:T(1024)}, f32[3072]{0:T(1024)S(1)}, bf16[256,3072]{1,0:T(8,128)(2,1)}) fusion(f32[272,3072]{1,0:T(8,128)S(1)} %copy-done.4, f32[256,1024]{1,0:T(8,128)S(1)} %copy-done.23, f32[256,1024]{1,0:T(8,128)S(1)} %copy-done.21, f32[256,1024]{1,0:T(8,128)S(1)} %copy-done.19, ...), kind=kLoop, calls=%fused_computation.30 | loop fusion | flops 14146560 | bytes 20521984 | tf_op jit(solution)/shard_map/reduce_sum | solution.py:259
  459.0 7.0 %multiply_reduce_fusion.6 = (f32[1024]{0:T(1024)}, f32[256]{0:T(256)}, f32[256]{0:T(256)}, f32[256,1024]{1,0:T(8,128)}) fusion(f32[272,1024]{1,0:T(8,128)} %get-tuple-element.118, f32[1024]{0:T(1024)} %bitcast.178, bf16[256,3072]{1,0:T(8,128)(2,1)} %get-tuple-element.114, bf16[3072,1024]{1,0:T(8,128)(2,1)} %bitcast.133), kind=kOutput, calls=%fused_computation.69 | convolution fusion | flops 1612184064 | bytes 9971712 | tf_op jit(solution)/shard_map/dot_general | solution.py:262
  471.8 4.5 convolution_convert_fusion.2.refs_0_
  476.2 58.8 %reduce_4.1 = (f32[768,128]{1,0:T(8,128)}, f32[256,128]{1,0:T(8,128)}, f32[32,128]{1,0:T(8,128)}) custom-call(bf16[3072,1024]{1,0:T(8,128)(2,1)} %convolution_convert_fusion.2.refs_0_, bf16[1024,1024]{1,0:T(8,128)(2,1)} %convolution_convert_fusion.3.refs_1_, f32[128,1024]{1,0:T(8,128)} %reshape.362.refs_2_), custom_call_target="tpu_custom_call" | custom-call | bytes 71303168 | tf_op jit(solution)/shard_map/reduce_4/pallas_call | solution.py:622
  542.4 16.2 %spread_5.1 = f32[2,2,2,4,40,128]{5,4,3,2,1,0:T(8,128)} custom-call(f32[40,128]{1,0:T(8,128)} %concatenate.45.part_ref), custom_call_target="tpu_custom_call" | custom-call | tf_op jit(solution)/shard_map/spread_5/pallas_call | solution.py:679
  (342 shorter events, 158.6 us)
Async XLA Ops:
  0.7 75.1 %copy-start.27 = (bf16[256,1024]{1,0:T(8,128)(2,1)S(1)}, bf16[256,1024]{1,0:T(8,128)(2,1)}, u32[]{:S(2)}) copy-start(bf16[256,1024]{1,0:T(8,128)(2,1)} %param.34) | copy-start | bytes 1572868
  0.7 27.4 %copy-start.51 = (f32[3,256,128]{2,1,0:T(8,128)S(1)}, f32[3,256,128]{2,1,0:T(8,128)}, u32[]{:S(2)}) copy-start(f32[3,256,128]{2,1,0:T(8,128)} %param.56) | copy-start | bytes 1179652
  0.7 27.4 %copy-start.66 = (f32[256,128]{1,0:T(8,128)S(1)}, f32[256,128]{1,0:T(8,128)}, u32[]{:S(2)}) copy-start(f32[256,128]{1,0:T(8,128)} %param.59) | copy-start | bytes 393220
  2.2 73.6 %collective-permute-start = (bf16[16,1024]{1,0:T(8,128)(2,1)}, bf16[16,1024]{1,0:T(8,128)(2,1)S(1)}, u32[]{:S(2)}, u32[]{:S(2)}) collective-permute-start(bf16[16,1024]{1,0:T(8,128)(2,1)} %slice.120), channel_id=1, source_target_pairs={{0,1},{1,2},{2,3},{4,5},{5,6},{6,7},{8,9},{9,10},{10,11},{12,13},{... | collective-permute-start | bytes 98312 | tf_op jit(solution)/shard_map/ppermute | solution.py:146
  8.9 69.3 %copy-start.82 = (f32[1,1024]{1,0:T(1,128)}, f32[1,1024]{1,0:T(1,128)S(1)}, u32[]{:S(2)}) copy-start(f32[1,1024]{1,0:T(1,128)S(1)} %get-tuple-element.128) | copy-start | bytes 12292
  9.8 70.4 %copy-start.74 = (f32[3,1,1024]{2,1,0:T(1,128)}, f32[3,1,1024]{2,1,0:T(1,128)S(1)}, u32[]{:S(2)}) copy-start(f32[3,1,1024]{2,1,0:T(1,128)S(1)} %get-tuple-element.123) | copy-start | bytes 36868
  9.8 70.4 %copy-start.75 = (f32[3,1,1024]{2,1,0:T(1,128)}, f32[3,1,1024]{2,1,0:T(1,128)S(1)}, u32[]{:S(2)}) copy-start(f32[3,1,1024]{2,1,0:T(1,128)S(1)} %get-tuple-element.124) | copy-start | bytes 36868
  10.4 17.8 %copy-start.85 = (f32[1024]{0:T(1024)}, f32[1024]{0:T(1024)S(1)}, u32[]{:S(2)}) copy-start(f32[1024]{0:T(1024)S(1)} %get-tuple-element.147) | copy-start | bytes 12292
  18.8 61.4 %copy-start.38 = (f32[1024,64]{0,1:T(8,128)}, f32[1024,64]{0,1:T(8,128)S(1)}, u32[]{:S(2)}) copy-start(f32[1024,64]{0,1:T(8,128)S(1)} %get-tuple-element.141) | copy-start | bytes 786436
  84.8 23.4 %all-to-all-start = ((bf16[256,4,256]{2,0,1:T(8,128)(2,1)}), bf16[256,4,256]{2,0,1:T(8,128)(2,1)S(1)}, u32[]{:S(2)}, u32[]{:S(2)}) async-start(bf16[256,4,256]{2,0,1:T(8,128)(2,1)} %bitcast.126), calls=%async_computation | async-start | bytes 1048576 | tf_op jit(solution)/shard_map/all_to_all | solution.py:190
  125.2 106.6 %copy-start.87 = (f32[272]{0:T(512)S(1)}, f32[272]{0:T(512)}, u32[]{:S(2)}) copy-start(f32[272]{0:T(512)} %copy-done.86) | copy-start | bytes 3268
  125.2 115.5 %all-to-all-start.1 = ((bf16[4,256,256]{2,1,0:T(8,128)(2,1)}), bf16[4,256,256]{2,1,0:T(8,128)(2,1)}, u32[]{:S(2)}, u32[]{:S(2)}) async-start(bf16[4,256,256]{2,1,0:T(8,128)(2,1)} %bitcast.170), calls=%async_computation.1 | async-start | bytes 1048576 | tf_op jit(solution)/shard_map/all_to_all | solution.py:195
  272.5 118.1 %all-to-all-start.2 = ((bf16[256,4,256]{2,0,1:T(8,128)(2,1)}), bf16[256,4,256]{2,0,1:T(8,128)(2,1)}, u32[]{:S(2)}, u32[]{:S(2)}) async-start(bf16[256,4,256]{2,0,1:T(8,128)(2,1)} %bitcast.125), calls=%async_computation.2 | async-start | bytes 1048576 | tf_op jit(solution)/shard_map/all_to_all | solution.py:190
  297.2 86.6 %copy-start.96 = (f32[256,4096]{1,0:T(8,128)S(1)}, f32[256,4096]{1,0:T(8,128)}, u32[]{:S(2)}) copy-start(f32[256,4096]{1,0:T(8,128)} %fusion.130) | copy-start | bytes 12582916
  408.2 27.7 %all-to-all-start.3 = ((bf16[4,256,256]{2,1,0:T(8,128)(2,1)}), bf16[4,256,256]{2,1,0:T(8,128)(2,1)}, u32[]{:S(2)}, u32[]{:S(2)}) async-start(bf16[4,256,256]{2,1,0:T(8,128)(2,1)} %bitcast.169), calls=%async_computation.3 | async-start | bytes 1048576 | tf_op jit(solution)/shard_map/all_to_all | solution.py:195
  412.4 15.2 %copy-start.61 = (f32[1024,16]{0,1:T(8,128)S(1)}, f32[1024,16]{0,1:T(8,128)}, u32[]{:S(2)}) copy-start(f32[1024,16]{0,1:T(8,128)} %copy-done.60) | copy-start | bytes 196612
  440.2 7.0 %collective-permute-start.1 = (f32[8,3072]{1,0:T(8,128)}, f32[8,3072]{1,0:T(8,128)}, u32[]{:S(2)}, u32[]{:S(2)}) collective-permute-start(f32[8,3072]{1,0:T(8,128)} %slice.172), channel_id=1, source_target_pairs={{1,0},{2,1},{3,2},{5,4},{6,5},{7,6},{9,8},{10,9},{11,10},{13,12},{... | collective-permute-start | bytes 294920 | tf_op jit(solution)/shard_map/ppermute | solution.py:249
  535.1 40.3 %copy-start.50 = (f32[768,128]{1,0:T(8,128)S(1)}, f32[768,128]{1,0:T(8,128)}, u32[]{:S(2)}) copy-start(f32[768,128]{1,0:T(8,128)} %get-tuple-element.55) | copy-start | bytes 1179652
  535.1 42.8 %copy-start.88 = (f32[2,1024]{1,0:T(2,128)S(1)}, f32[2,1024]{1,0:T(2,128)}, u32[]{:S(2)}) copy-start(f32[2,1024]{1,0:T(2,128)} %param.39) | copy-start | bytes 24580
  536.9 42.6 %copy-start.93 = (f32[1024]{0:T(1024)S(1)}, f32[1024]{0:T(1024)}, u32[]{:S(2)}) copy-start(f32[1024]{0:T(1024)} %param.45) | copy-start | bytes 12292
  560.2 24.0 %copy-start.45 = (f32[1024,128]{1,0:T(8,128)S(1)}, f32[1024,128]{1,0:T(8,128)}, u32[]{:S(2)}) copy-start(f32[1024,128]{1,0:T(8,128)} %param.62) | copy-start | bytes 1572868
  560.2 24.0 %copy-start.48 = (f32[1024,128]{1,0:T(8,128)S(1)}, f32[1024,128]{1,0:T(8,128)}, u32[]{:S(2)}) copy-start(f32[1024,128]{1,0:T(8,128)} %get-tuple-element.57) | copy-start | bytes 1572868
  564.2 22.7 %copy-start.46 = (f32[1024,128]{1,0:T(8,128)S(1)}, f32[1024,128]{1,0:T(8,128)}, u32[]{:S(2)}) copy-start(f32[1024,128]{1,0:T(8,128)} %param.65) | copy-start | bytes 1572868
  564.2 22.7 %copy-start.47 = (f32[1024,128]{1,0:T(8,128)S(1)}, f32[1024,128]{1,0:T(8,128)}, u32[]{:S(2)}) copy-start(f32[1024,128]{1,0:T(8,128)} %get-tuple-element.58) | copy-start | bytes 1572868
  (83 other events, 521.6 us)
